TPU v7x, 32 devices: a 4x2x2 block of a 4x4x8 slice. The times are simulated.
32 devices in a mesh: dp: 4 (over y, z), sp: 8 (over x, core).
Axes of the slice: x: 4, y: 2, z: 2, core: 2. Of those that a mesh axis runs over, the one named last changes fastest.
The devices are a block of a 4x4x8 slice.
Arguments:
- x_one: bfloat16 [2048, 7168], P(('dp', 'sp')), parts along dimension 0
- seg_one: int32 [2048], P(('dp', 'sp')), parts along dimension 0
- pos_one: int32 [2048], P(('dp', 'sp')), parts along dimension 0
- x_two: bfloat16 [2048, 7168], P(('dp', 'sp')), parts along dimension 0
- seg_two: int32 [2048], P(('dp', 'sp')), parts along dimension 0
- pos_two: int32 [2048], P(('dp', 'sp')), parts along dimension 0
- w_qdown: bfloat16 [7168, 1536], replicated
- gain_q: bfloat16 [1536], replicated
- w_qup: bfloat16 [1536, 12288], replicated
- w_kvdown: bfloat16 [7168, 576], replicated
- gain_kv: bfloat16 [512], replicated
- w_kvup: bfloat16 [512, 16384], replicated
- w_out: bfloat16 [8192, 7168], replicated
Outputs:
- output 1: bfloat16 [2048, 7168], P(('dp', 'sp')), parts along dimension 0
- output 2: bfloat16 [2048, 7168], P(('dp', 'sp')), parts along dimension 0
There are 4 independent parts. A program takes and returns all parts, laid end to end along the dimension named above; an argument that names none is the same for every part.
All inputs are finite; a program needn't handle non-finite values.
Results may differ from a plain program's by a relative error of at most 0.0139229.
Values are sent between devices in bfloat16 or wider.
A program may use at most 768 MiB of HBM per device.

v0:
```python
import functools

import jax
import jax.numpy as jnp
from jax import lax
from jax.experimental import pallas as pl
from jax.experimental.pallas import tpu as pltpu
from jax.sharding import PartitionSpec as P

NOPE_DIM = 128
ROPE_DIM = 64
HALF_ROPE = 32
KV_LAT = 512
Q_LAT = 1536
V_DIM = 128
QK_DIM = NOPE_DIM + ROPE_DIM
KV_DIM = NOPE_DIM + V_DIM
ROPE_BASE = 10000.0
NORM_EPS = 1e-6
LANES = 128

DOWN_ROWS = 1024
QD_SLOTS = 4
QU_HEADS = 4
QU_SLOTS = 3
KU_HEADS = 4
KU_SLOTS = 2
WO_ROWS = 2048
WO_COLS = 512
WO_SLOTS = 6
KVW = KV_LAT + LANES
MASKED = -1e30
BIG = 3e38
F32 = jnp.float32
BF16 = jnp.bfloat16


def body(n_sp, heads, d_model, blk,
         x_one, x_two, tab, w_qd, gain_q, w_qu, w_kvd, gain_kv, w_kvu, w_out,
         y_one, y_two,
         x_all, tab_all, kvd, qd, qu, ku, wo, acc_kv, acc_q, kv_all, cq_all,
         cap, kr, q_s, kvs, o_all, acc_y, y_st,
         x_sem, tab_sem, tab_ss, tab_rs, kvd_sem, qd_sem, qu_sem, ku_sem, wo_sem,
         kv_ss, kv_rs, cq_ss, cq_rs, o_ss, o_rs, y_ls, y_ss, y_rs):
    n_chip = n_sp // 2
    me = lax.axis_index("sp")
    core = lax.rem(me, 2)
    chip = me // 2
    pair = me + 1 - 2 * core
    right = lax.rem(me + 2, n_sp)
    left = lax.rem(me + n_sp - 2, n_sp)
    opp = lax.rem(me + 4, n_sp)
    q_rows = 2 * blk
    toks = n_sp * blk
    half_heads = heads // 2
    y_cols = d_model // 2
    n_down = d_model // DOWN_ROWS
    n_qu = half_heads // QU_HEADS
    n_ku = half_heads // KU_HEADS
    n_wo_k = heads * V_DIM // WO_ROWS
    n_wo_n = y_cols // WO_COLS
    n_wo = n_wo_k * n_wo_n

    def rcopy(src, dst, ss, rs, dev):
        return pltpu.make_async_remote_copy(
            src_ref=src, dst_ref=dst, send_sem=ss, recv_sem=rs,
            device_id={"sp": dev}, device_id_type=pl.DeviceIdType.MESH)

    x_in = (x_one, x_two)
    x_cp = [pltpu.make_async_copy(x_in[m], x_all.at[pl.ds(m * blk, blk)], x_sem.at[m]) for m in range(2)]
    for c in x_cp:
        c.start()

    def kvd_copy(k):
        rows = pl.ds(pl.multiple_of(k * DOWN_ROWS, DOWN_ROWS), DOWN_ROWS)
        return pltpu.make_async_copy(w_kvd.at[rows], kvd.at[rows], kvd_sem.at[k])

    def qd_copy(k):
        rows = pl.ds(pl.multiple_of(k * DOWN_ROWS, DOWN_ROWS), DOWN_ROWS)
        slot = lax.rem(k, QD_SLOTS)
        return pltpu.make_async_copy(w_qd.at[rows], qd.at[slot], qd_sem.at[slot])

    def qu_copy(i):
        width = QU_HEADS * QK_DIM
        cols = pl.ds(pl.multiple_of(core * (half_heads * QK_DIM) + i * width, LANES), width)
        slot = lax.rem(i, QU_SLOTS)
        return pltpu.make_async_copy(w_qu.at[:, cols], qu.at[slot], qu_sem.at[slot])

    def ku_copy(i):
        width = KU_HEADS * KV_DIM
        cols = pl.ds(pl.multiple_of(core * (half_heads * KV_DIM) + i * width, LANES), width)
        slot = lax.rem(i, KU_SLOTS)
        return pltpu.make_async_copy(w_kvu.at[:, cols], ku.at[slot], ku_sem.at[slot])

    def wo_copy(g):
        n = g // n_wo_k
        k = lax.rem(g, n_wo_k)
        rows = pl.ds(pl.multiple_of(k * WO_ROWS, WO_ROWS), WO_ROWS)
        cols = pl.ds(pl.multiple_of(core * y_cols + n * WO_COLS, LANES), WO_COLS)
        slot = lax.rem(g, WO_SLOTS)
        return pltpu.make_async_copy(w_out.at[rows, cols], wo.at[slot], wo_sem.at[slot])

    for k in range(n_down):
        kvd_copy(k).start()
    for k in range(QD_SLOTS):
        qd_copy(k).start()

    barrier = pltpu.get_barrier_semaphore()
    for dev in (pair, left, right):
        pl.semaphore_signal(barrier, inc=1, device_id={"sp": dev}, device_id_type=pl.DeviceIdType.MESH)
    pl.semaphore_wait(barrier, 3)

    def my_rows(m, c):
        return pl.ds(pl.multiple_of(m * q_rows + c * blk, blk), blk)

    tab_cp = [pltpu.make_async_copy(tab.at[pl.ds(m * blk, blk)], tab_all.at[my_rows(m, core)], tab_sem.at[m]) for m in range(2)]
    tab_rc = [rcopy(tab.at[pl.ds(m * blk, blk)], tab_all.at[my_rows(m, core)], tab_ss.at[m], tab_rs.at[m], pair) for m in range(2)]
    for m in range(2):
        tab_cp[m].start()
        tab_rc[m].start()
    for c in x_cp:
        c.wait()

    acc_kv[...] = jnp.zeros_like(acc_kv)

    def kv_step(k, carry):
        kvd_copy(k).wait()
        rows = pl.ds(pl.multiple_of(k * DOWN_ROWS, DOWN_ROWS), DOWN_ROWS)
        acc_kv[...] += jnp.dot(x_all[:, rows], kvd[rows, :], preferred_element_type=F32)
        return carry

    lax.fori_loop(0, n_down, kv_step, 0)
    for m in range(2):
        tab_cp[m].wait()

    lane = lax.broadcasted_iota(jnp.int32, (blk, LANES), 1)
    first_half = lax.rem(lane, ROPE_DIM) < HALF_ROPE

    def rotate(z, cos, sin, sel):
        swapped = jnp.where(sel, pltpu.roll(z, LANES - HALF_ROPE, 1), pltpu.roll(z, HALF_ROPE, 1))
        return z * cos + swapped * sin

    for m in range(2):
        rows = pl.ds(m * blk, blk)
        lat = acc_kv[rows, :KV_LAT]
        inv = lax.rsqrt(jnp.mean(lat * lat, axis=-1, keepdims=True) + NORM_EPS)
        own = pl.ds(pl.multiple_of(me * blk, blk), blk)
        kv_all[m, own, :KV_LAT] = (lat * inv * gain_kv[...].astype(F32)).astype(BF16)
        raw = acc_kv[rows, KV_LAT:]
        raw = jnp.concatenate([raw, raw], axis=1)
        t = tab_all[my_rows(m, core), :]
        kv_all[m, own, KV_LAT:] = rotate(raw, t[:, :LANES], t[:, LANES:2 * LANES], first_half).astype(BF16)

    def piece(m, dev):
        return kv_all.at[m, pl.ds(pl.multiple_of(dev * blk, blk), blk)]

    def kv_send(i, m, src_dev, role, dev):
        return rcopy(piece(m, src_dev), piece(m, src_dev), kv_ss.at[i], kv_rs.at[role, m], dev)

    def kv_wait(m, src_dev, role):
        rcopy(piece(m, src_dev), piece(m, src_dev), kv_ss.at[0], kv_rs.at[role, m], pair).wait_recv()

    sends = []
    for m in range(2):
        sends.append(kv_send(len(sends), m, me, 2, left))
        sends.append(kv_send(len(sends), m, me, 1, right))
    for m in range(2):
        sends.append(kv_send(len(sends), m, me, 0, pair))
    for c in sends:
        c.start()

    acc_q[...] = jnp.zeros_like(acc_q)

    def q_step(k, carry):
        qd_copy(k).wait()
        rows = pl.ds(pl.multiple_of(k * DOWN_ROWS, DOWN_ROWS), DOWN_ROWS)
        acc_q[...] += jnp.dot(x_all[:, rows], qd[lax.rem(k, QD_SLOTS)], preferred_element_type=F32)

        @pl.when(k + QD_SLOTS < n_down)
        def _():
            qd_copy(k + QD_SLOTS).start()

        return carry

    n_first = n_down - QD_SLOTS
    lax.fori_loop(0, n_first, q_step, 0)
    for i in range(QU_SLOTS):
        qu_copy(i).start()
    for i in range(KU_SLOTS):
        ku_copy(i).start()
    for g in range(WO_SLOTS):
        wo_copy(g).start()
    lax.fori_loop(n_first, n_down, q_step, 0)

    for m in range(2):
        rows = pl.ds(m * blk, blk)
        lat = acc_q[rows, :]
        inv = lax.rsqrt(jnp.mean(lat * lat, axis=-1, keepdims=True) + NORM_EPS)
        cq_all[my_rows(m, core), :] = (lat * inv * gain_q[...].astype(F32)).astype(BF16)
    cq_rc = [rcopy(cq_all.at[my_rows(m, core)], cq_all.at[my_rows(m, core)], cq_ss.at[m], cq_rs.at[m], pair) for m in range(2)]
    for c in cq_rc:
        c.start()

    second = []
    for m in range(2):
        kv_wait(m, left, 1)
        kv_wait(m, right, 2)
    second.append(kv_send(6, 0, left, 3, right))
    second.append(kv_send(7, 1, right, 3, left))
    for m in range(2):
        second.append(kv_send(8 + m, m, left, 4, pair))
        second.append(kv_send(10 + m, m, right, 5, pair))
    for c in second:
        c.start()
    sends += second

    for m in range(2):
        tab_rc[m].wait_recv()
    for m in range(2):
        start = tab_all[m * q_rows:(m + 1) * q_rows, 2 * LANES:]
        start = jnp.concatenate([start] * (toks // LANES), axis=1)
        key = lax.broadcasted_iota(jnp.int32, (q_rows, toks), 1)
        query = lax.broadcasted_iota(jnp.int32, (q_rows, toks), 0) + chip * q_rows
        keep = (key <= query) & (key.astype(F32) >= start)
        cap[m] = jnp.where(keep, BIG, MASKED)
    for c in cq_rc:
        c.wait_recv()

    lane2 = lax.broadcasted_iota(jnp.int32, (2 * q_rows, LANES), 1)
    low = lane2 < ROPE_DIM
    first_half2 = lax.rem(lane2, ROPE_DIM) < HALF_ROPE

    def qu_step(i, carry):
        qu_copy(i).wait()
        f = jnp.dot(cq_all[...], qu[lax.rem(i, QU_SLOTS)], preferred_element_type=F32)
        cos = tab_all[:, :LANES]
        sin = tab_all[:, LANES:2 * LANES]
        for p in range(QU_HEADS // 2):
            base = 2 * QK_DIM * p
            t0 = f[:, base:base + LANES]
            t1 = f[:, base + LANES:base + 2 * LANES]
            t2 = f[:, base + 2 * LANES:base + 3 * LANES]
            q_s[i, :, base:base + LANES] = t0.astype(BF16)
            q_s[i, :, base + LANES:base + 2 * LANES] = pltpu.roll(jnp.where(low, t2, t1), ROPE_DIM, 1).astype(BF16)
            q_s[i, :, base + 2 * LANES:base + 3 * LANES] = rotate(jnp.where(low, t1, t2), cos, sin, first_half2).astype(BF16)

        @pl.when(i + QU_SLOTS < n_qu)
        def _():
            qu_copy(i + QU_SLOTS).start()

        return carry

    lax.fori_loop(0, n_qu // 2, qu_step, 0)
    third = []
    for m in range(2):
        kv_wait(m, opp, 3)
        third.append(kv_send(12 + m, m, opp, 6, pair))
    for c in third:
        c.start()
    sends += third
    lax.fori_loop(n_qu // 2, n_qu, qu_step, 0)

    other = 1 - 2 * core
    for m in range(2):
        kv_wait(m, pair, 0)
        kv_wait(m, left + other, 4)
        kv_wait(m, right + other, 5)
        kv_wait(m, opp + other, 6)
    lane3 = lax.broadcasted_iota(jnp.int32, (toks, LANES), 1)
    for m in range(2):
        t = kv_all[m, :, KV_LAT:].astype(F32)
        kr[0, m] = jnp.where(lane3 < ROPE_DIM, t, 0.0).astype(BF16)
        kr[1, m] = jnp.where(lane3 < ROPE_DIM, 0.0, t).astype(BF16)

    exp_scale = QK_DIM ** -0.5 * 1.4426950408889634

    def o_copy(i):
        width = KU_HEADS * V_DIM
        cols = pl.ds(pl.multiple_of(core * (half_heads * V_DIM) + i * width, LANES), width)
        return rcopy(o_all.at[:, cols], o_all.at[:, cols], o_ss.at[i], o_rs.at[i], pair)

    def at_step(i, carry):
        ku_copy(i).wait()
        w = ku.at[lax.rem(i, KU_SLOTS)]
        for m in range(2):
            for r in range(toks // 256):
                kvs[m, r * 256:(r + 1) * 256, :] = jnp.dot(
                    kv_all[m, r * 256:(r + 1) * 256, :KV_LAT], w[...], preferred_element_type=F32).astype(BF16)

        @pl.when(i + KU_SLOTS < n_ku)
        def _():
            ku_copy(i + KU_SLOTS).start()

        for m in range(2):
            rows = slice(m * q_rows, (m + 1) * q_rows)
            for j in range(KU_HEADS):
                base = 2 * QK_DIM * (j // 2)
                nope = q_s[i, rows, base + LANES * (j % 2):base + LANES * (j % 2) + LANES]
                rope = q_s[i, rows, base + 2 * LANES:base + 3 * LANES]
                qc = jnp.concatenate([nope, rope], axis=1)
                kc = jnp.concatenate([kvs[m, :, KV_DIM * j:KV_DIM * j + NOPE_DIM], kr[j % 2, m]], axis=1)
                s = lax.dot_general(qc, kc, (((1,), (1,)), ((), ())), preferred_element_type=F32)
                s = jnp.minimum(s, cap[m])
                top = jnp.max(s, axis=-1, keepdims=True)
                e = jnp.exp2((s - top) * exp_scale)
                inv = 1.0 / jnp.sum(e, axis=-1, keepdims=True)
                p = (e * inv).astype(BF16)
                v = kvs[m, :, KV_DIM * j + NOPE_DIM:KV_DIM * (j + 1)]
                o = jnp.dot(p, v, preferred_element_type=F32).astype(BF16)
                col = pl.multiple_of(core * (half_heads * V_DIM) + i * (KU_HEADS * V_DIM) + j * V_DIM, LANES)
                o_all[rows, pl.ds(col, V_DIM)] = o
        o_copy(i).start()
        return carry

    lax.fori_loop(0, n_ku, at_step, 0)

    width = KU_HEADS * V_DIM
    for i in range(n_ku):
        cols = pl.ds(pl.multiple_of((1 - core) * (half_heads * V_DIM) + i * width, LANES), width)
        rcopy(o_all.at[:, cols], o_all.at[:, cols], o_ss.at[i], o_rs.at[i], pair).wait_recv()

    y_out = (y_one, y_two)

    def y_copies(n):
        slot = lax.rem(n, 2)
        cols = pl.ds(pl.multiple_of(core * y_cols + n * WO_COLS, LANES), WO_COLS)
        local = [pltpu.make_async_copy(y_st.at[slot, my_rows(m, core)], y_out[m].at[:, cols], y_ls.at[slot, m]) for m in range(2)]
        remote = [rcopy(y_st.at[slot, my_rows(m, 1 - core)], y_out[m].at[:, cols], y_ss.at[slot, m], y_rs.at[n, m], pair) for m in range(2)]
        return local, remote

    def y_wait(n):
        local, remote = y_copies(n)
        for m in range(2):
            local[m].wait()
            remote[m].wait_send()

    def wo_step(n, carry):
        for k in range(n_wo_k):
            g = n * n_wo_k + k
            wo_copy(g).wait()
            d = jnp.dot(o_all[:, k * WO_ROWS:(k + 1) * WO_ROWS], wo[lax.rem(g, WO_SLOTS)], preferred_element_type=F32)
            if k == 0:
                acc_y[...] = d
            else:
                acc_y[...] += d

            @pl.when(g + WO_SLOTS < n_wo)
            def _():
                wo_copy(g + WO_SLOTS).start()

        @pl.when(n >= 2)
        def _():
            y_wait(n - 2)

        y_st[lax.rem(n, 2)] = acc_y[...].astype(BF16)
        local, remote = y_copies(n)
        for m in range(2):
            local[m].start()
            remote[m].start()
        return carry

    lax.fori_loop(0, n_wo_n, wo_step, 0)
    y_wait(n_wo_n - 2)
    y_wait(n_wo_n - 1)
    for n in range(n_wo_n):
        cols = pl.ds(pl.multiple_of((1 - core) * y_cols + n * WO_COLS, LANES), WO_COLS)
        for m in range(2):
            rcopy(y_st.at[0, my_rows(m, core)], y_out[m].at[:, cols], y_ss.at[0, m], y_rs.at[n, m], pair).wait_recv()
    for m in range(2):
        tab_rc[m].wait_send()
        cq_rc[m].wait_send()
    for c in sends:
        c.wait_send()
    for i in range(n_ku):
        o_copy(i).wait_send()


def mla(n_sp, x_one, x_two, tab, w_qd, gain_q, w_qu, w_kvd, gain_kv, w_kvu, w_out):
    blk, d_model = x_one.shape
    heads = w_out.shape[0] // V_DIM
    toks = n_sp * blk
    q_rows = 2 * blk
    n_down = d_model // DOWN_ROWS
    n_qu = heads // 2 // QU_HEADS
    n_ku = heads // 2 // KU_HEADS
    n_wo_n = d_model // 2 // WO_COLS
    hbm = pl.BlockSpec(memory_space=pl.ANY)
    vmem = pl.BlockSpec(memory_space=pltpu.VMEM)
    dma = pltpu.SemaphoreType.DMA
    return pl.pallas_call(
        functools.partial(body, n_sp, heads, d_model, blk),
        out_shape=[jax.ShapeDtypeStruct((blk, d_model), BF16)] * 2,
        in_specs=[hbm, hbm, hbm, hbm, vmem, hbm, hbm, vmem, hbm, hbm],
        out_specs=[hbm, hbm],
        scratch_shapes=[
            pltpu.VMEM((2 * blk, d_model), BF16),
            pltpu.VMEM((2 * q_rows, 3 * LANES), F32),
            pltpu.VMEM((d_model, KV_LAT + ROPE_DIM), BF16),
            pltpu.VMEM((QD_SLOTS, DOWN_ROWS, Q_LAT), BF16),
            pltpu.VMEM((QU_SLOTS, Q_LAT, QU_HEADS * QK_DIM), BF16),
            pltpu.VMEM((KU_SLOTS, KV_LAT, KU_HEADS * KV_DIM), BF16),
            pltpu.VMEM((WO_SLOTS, WO_ROWS, WO_COLS), BF16),
            pltpu.VMEM((2 * blk, KV_LAT + ROPE_DIM), F32),
            pltpu.VMEM((2 * blk, Q_LAT), F32),
            pltpu.VMEM((2, toks, KVW), BF16),
            pltpu.VMEM((2 * q_rows, Q_LAT), BF16),
            pltpu.VMEM((2, q_rows, toks), F32),
            pltpu.VMEM((2, 2, toks, LANES), BF16),
            pltpu.VMEM((n_qu, 2 * q_rows, QU_HEADS * QK_DIM), BF16),
            pltpu.VMEM((2, toks, KU_HEADS * KV_DIM), BF16),
            pltpu.VMEM((2 * q_rows, heads * V_DIM), BF16),
            pltpu.VMEM((2 * q_rows, WO_COLS), F32),
            pltpu.VMEM((2, 2 * q_rows, WO_COLS), BF16),
            dma((2,)), dma((2,)), dma((2,)), dma((2,)),
            dma((n_down,)), dma((QD_SLOTS,)), dma((QU_SLOTS,)), dma((KU_SLOTS,)), dma((WO_SLOTS,)),
            dma((14,)), dma((7, 2)),
            dma((2,)), dma((2,)),
            dma((n_ku,)), dma((n_ku,)),
            dma((2, 2)), dma((2, 2)), dma((n_wo_n, 2)),
        ],
        compiler_params=pltpu.CompilerParams(
            collective_id=0, has_side_effects=True, vmem_limit_bytes=67043328),
        name="mla",
    )(x_one, x_two, tab, w_qd, gain_q, w_qu, w_kvd, gain_kv, w_kvu, w_out)


def solution(mesh):
    tok_spec = P(('dp', 'sp'), None)
    idx_spec = P(('dp', 'sp'))
    n_sp = mesh.shape['sp']

    def table(pos):
        blk = pos.shape[0]
        inv_freq = ROPE_BASE ** (-jnp.arange(HALF_ROPE, dtype=F32) / HALF_ROPE)
        ang = pos.astype(F32)[:, None] * inv_freq
        cos, sin = jnp.cos(ang), jnp.sin(ang)
        start = lax.axis_index('sp') * blk + jnp.arange(blk, dtype=jnp.int32) - pos
        start = jnp.broadcast_to(start.astype(F32)[:, None], (blk, LANES))
        return jnp.concatenate([cos] * 4 + [-sin, sin] * 2 + [start], axis=1)

    def local_body(x_one, seg_one, pos_one, x_two, seg_two, pos_two, w_qdown, gain_q, w_qup, w_kvdown, gain_kv, w_kvup, w_out):
        tab = jnp.concatenate([table(pos_one), table(pos_two)], axis=0)
        return mla(n_sp, x_one, x_two, tab, w_qdown, gain_q.reshape(1, -1), w_qup, w_kvdown, gain_kv.reshape(1, -1), w_kvup, w_out)

    return jax.shard_map(local_body, mesh=mesh, in_specs=(tok_spec, idx_spec, idx_spec, tok_spec, idx_spec, idx_spec) + (P(),) * 7, out_specs=(tok_spec, tok_spec), check_vma=False)
```

profile of v0, /device:TPU:81, one launch (start us, length us, event | category | flops | bytes accessed | tf_op | source)
XLA Modules:
  0.0 107.7 jit_solution(13392918043890825842)
XLA Ops:
  0.6 0.7 subtract_convert_fusion
  1.4 1.3 %reshape.21.gain_kv = bf16[1,512]{1,0:T(2,128)(2,1)} reshape(bf16[512]{0:T(512)(128)(2,1)} %param.21) | data formatting | bytes 2048 | tf_op jit(solution)/shard_map/reshape | solution.py:443
  2.7 1.3 %reshape.20.gain_q = bf16[1,1536]{1,0:T(2,128)(2,1)} reshape(bf16[1536]{0:T(1024)(128)(2,1)} %param.18) | data formatting | bytes 6144 | tf_op jit(solution)/shard_map/reshape | solution.py:443
  3.9 0.1 broadcast_in_dim.5
  4.0 0.1 broadcast_in_dim.4
  4.1 0.3 multiply_sine_fusion.1
  4.4 0.1 concatenate.9
  4.5 0.1 concatenate.10
  4.7 0.7 pad_maximum_fusion.tab
  5.4 12.4 %copy.16.w_kvd = bf16[7168,576]{1,0:T(8,128)(2,1)} copy(bf16[7168,576]{0,1:T(8,128)(2,1)} %param.20) | data formatting | bytes 16515072 | tf_op args[9]
  17.8 85.6 %mla.1 = (bf16[64,7168]{1,0:T(8,128)(2,1)}, bf16[64,7168]{1,0:T(8,128)(2,1)}) custom-call(bf16[64,7168]{1,0:T(8,128)(2,1)} %x_one.1, bf16[64,7168]{1,0:T(8,128)(2,1)} %x_two.1, f32[128,384]{1,0:T(8,128)} %pad_maximum_fusion.tab, bf16[7168,1536]{1,0:T(8,128)(2,1)} %w_qd.1, bf16[1,1536]{1,0:T(2,128)(2,1)} %reshape.20.gain_q, bf16[1536,12288]{1,0:T(8,128)(2,1)} %w_qu.1, ...), custom_call_target="tpu_custom_call" | custom-call | tf_op jit(solution)/shard_map/mla/pallas_call | solution.py:390
  103.4 2.2 %copy.19 = bf16[64,7168]{1,0:T(8,128)(2,1)} copy(bf16[64,7168]{1,0:T(8,128)(2,1)} %get-tuple-element.19) | data formatting | bytes 1835008
  105.6 2.2 %copy.20 = bf16[64,7168]{1,0:T(8,128)(2,1)} copy(bf16[64,7168]{1,0:T(8,128)(2,1)} %get-tuple-element.20) | data formatting | bytes 1835008
  (1 shorter events, 0.0 us)
where the time goes:
time: 108 us
  Pallas kernels  85.6 us (79%)
  local copies, waits for them, and re-layouts  19.7 us (18%)
  other arithmetic  1.76 us (2%)
    pallas_call x1, Pallas kernels, mla(): pl.pallas_call(functools.partial(body, n_sp, heads, d_model, blk), out_sh...  85.6 us
    unnamed x3, local copies, waits for them, and re-layouts  16.7 us

commit v1 on v0

v1 whole, which is shorter than its diff:
```python
import functools

import jax
import jax.numpy as jnp
import numpy as np
from jax import lax
from jax.experimental import pallas as pl
from jax.experimental.pallas import tpu as pltpu
from jax.sharding import PartitionSpec as P

NOPE_DIM = 128
ROPE_DIM = 64
HALF_ROPE = 32
KV_LAT = 512
Q_LAT = 1536
V_DIM = 128
QK_DIM = NOPE_DIM + ROPE_DIM
KV_DIM = NOPE_DIM + V_DIM
ROPE_BASE = 10000.0
NORM_EPS = 1e-6
LANES = 128

ROWS = 1024
COLS = 512
RING = 26
QU_HEADS = 4
QU_SLOTS = 2
KU_HEADS = 2
KU_SLOTS = 4
KVW = KV_LAT + LANES
MASKED = -1e30
BIG = 3e38
F32 = jnp.float32
BF16 = jnp.bfloat16


def body(n_sp, heads, d_model, blk,
         x_one, x_two, pos, freq, w_qd, gain_q, w_qu, w_kvd, gain_kv, w_kvu, w_out,
         y_one, y_two,
         x_all, pos_all, trig, kvd, ring, qu, ku, acc_kv, acc_q, kv_all, cq_all,
         cap, kr, q_s, kvs0, kvs1, s0, s1, p0, p1, o_all, acc_y, y_st,
         x_sem, pos_sem, pos_ss, pos_rs, kvd_sem, ring_sem, qu_sem, ku_sem,
         kv_ss, kv_rs, cq_ss, cq_rs, o_ss, o_rs, y_ls, y_ss, y_rs):
    me = lax.axis_index("sp")
    core = lax.rem(me, 2)
    chip = me // 2
    pair = me + 1 - 2 * core
    right = lax.rem(me + 2, n_sp)
    left = lax.rem(me + n_sp - 2, n_sp)
    opp = lax.rem(me + 4, n_sp)
    q_rows = 2 * blk
    toks = n_sp * blk
    half_heads = heads // 2
    y_cols = d_model // 2
    n_down = d_model // ROWS
    n_qd_c = Q_LAT // COLS
    n_qd = n_down * n_qd_c
    n_qu = half_heads // QU_HEADS
    n_ku = half_heads // KU_HEADS
    n_wo_k = heads * V_DIM // ROWS
    n_wo_n = y_cols // COLS
    n_wo = n_wo_k * n_wo_n

    def rcopy(src, dst, ss, rs, dev):
        return pltpu.make_async_remote_copy(
            src_ref=src, dst_ref=dst, send_sem=ss, recv_sem=rs,
            device_id={"sp": dev}, device_id_type=pl.DeviceIdType.MESH)

    def ds(start, size):
        return pl.ds(start if isinstance(start, int) else pl.multiple_of(start, size), size)

    def kvd_copy(k):
        return pltpu.make_async_copy(w_kvd.at[:, ds(k * ROWS, ROWS)], kvd.at[k], kvd_sem.at[k])

    def qd_copy(g):
        src = w_qd.at[ds(g // n_qd_c * ROWS, ROWS), ds(lax.rem(g, n_qd_c) * COLS, COLS)]
        return pltpu.make_async_copy(src, ring.at[g], ring_sem.at[g])

    def qu_copy(i):
        width = QU_HEADS * QK_DIM
        cols = ds(core * (half_heads * QK_DIM) + i * width, width)
        slot = lax.rem(i, QU_SLOTS)
        return pltpu.make_async_copy(w_qu.at[:, cols], qu.at[slot], qu_sem.at[slot])

    def ku_copy(i):
        width = KU_HEADS * KV_DIM
        cols = ds(core * (half_heads * KV_DIM) + i * width, width)
        slot = lax.rem(i, KU_SLOTS)
        return pltpu.make_async_copy(w_kvu.at[:, cols], ku.at[slot], ku_sem.at[slot])

    def wo_slot(g):
        return lax.rem(g + n_qd, RING)

    def wo_copy(g):
        rows = ds(lax.rem(g, n_wo_k) * ROWS, ROWS)
        cols = ds(core * y_cols + g // n_wo_k * COLS, COLS)
        return pltpu.make_async_copy(w_out.at[rows, cols], ring.at[wo_slot(g)], ring_sem.at[wo_slot(g)])

    x_in = (x_one, x_two)
    x_cp = [pltpu.make_async_copy(x_in[m], x_all.at[pl.ds(m * blk, blk)], x_sem.at[m]) for m in range(2)]
    for c in x_cp:
        c.start()
    for k in range(n_down):
        kvd_copy(k).start()
    for g in range(n_qd):
        qd_copy(g).start()

    barrier = pltpu.get_barrier_semaphore()
    for dev in (pair, left, right):
        pl.semaphore_signal(barrier, inc=1, device_id={"sp": dev}, device_id_type=pl.DeviceIdType.MESH)
    pl.semaphore_wait(barrier, 3)

    def my_rows(m, c):
        return ds(m * q_rows + c * blk, blk)

    pos_cp = [pltpu.make_async_copy(pos.at[pl.ds(m * blk, blk)], pos_all.at[my_rows(m, core)], pos_sem.at[m]) for m in range(2)]
    pos_rc = [rcopy(pos.at[pl.ds(m * blk, blk)], pos_all.at[my_rows(m, core)], pos_ss.at[m], pos_rs.at[m], pair) for m in range(2)]
    for m in range(2):
        pos_cp[m].start()
        pos_rc[m].start()

    for m in range(2):
        pos_cp[m].wait()
        pos_rc[m].wait_recv()
    lane2 = lax.broadcasted_iota(jnp.int32, (2 * q_rows, LANES), 1)
    first_half2 = lax.rem(lane2, ROPE_DIM) < HALF_ROPE
    ang = pos_all[...] * freq[...]
    trig[0] = jnp.cos(ang)
    sin = jnp.sin(ang)
    trig[1] = jnp.where(first_half2, -sin, sin)
    for m in range(2):
        row = lax.broadcasted_iota(jnp.int32, (q_rows, LANES), 0) + chip * q_rows
        start = row.astype(F32) - pos_all[m * q_rows:(m + 1) * q_rows, :]
        for c in range(toks // LANES):
            key = lax.broadcasted_iota(jnp.int32, (q_rows, LANES), 1) + c * LANES
            keep = (key <= row) & (key.astype(F32) >= start)
            cap[m, :, c * LANES:(c + 1) * LANES] = jnp.where(keep, BIG, MASKED)
    for c in x_cp:
        c.wait()

    acc_kv[...] = jnp.zeros_like(acc_kv)

    def kv_step(k, carry):
        kvd_copy(k).wait()
        acc_kv[...] += lax.dot_general(x_all[:, ds(k * ROWS, ROWS)], kvd[k], (((1,), (1,)), ((), ())), preferred_element_type=F32)
        return carry

    lax.fori_loop(0, n_down, kv_step, 0)

    lane = lax.broadcasted_iota(jnp.int32, (blk, LANES), 1)
    first_half = lax.rem(lane, ROPE_DIM) < HALF_ROPE

    def rotate(z, cos, sin, sel):
        swapped = jnp.where(sel, pltpu.roll(z, LANES - HALF_ROPE, 1), pltpu.roll(z, HALF_ROPE, 1))
        return z * cos + swapped * sin

    own = ds(me * blk, blk)
    for m in range(2):
        rows = pl.ds(m * blk, blk)
        lat = acc_kv[rows, :KV_LAT]
        inv = lax.rsqrt(jnp.mean(lat * lat, axis=-1, keepdims=True) + NORM_EPS)
        kv_all[m, own, :KV_LAT] = (lat * inv * gain_kv[...]).astype(BF16)
        raw = acc_kv[rows, KV_LAT:]
        raw = jnp.concatenate([raw, raw], axis=1)
        kv_all[m, own, KV_LAT:] = rotate(raw, trig[0, my_rows(m, core), :], trig[1, my_rows(m, core), :], first_half).astype(BF16)

    def piece(m, dev):
        return kv_all.at[m, ds(dev * blk, blk)]

    def kv_send(i, m, src_dev, role, dev):
        return rcopy(piece(m, src_dev), piece(m, src_dev), kv_ss.at[i], kv_rs.at[role, m], dev)

    def kv_wait(m, src_dev, role):
        rcopy(piece(m, src_dev), piece(m, src_dev), kv_ss.at[0], kv_rs.at[role, m], pair).wait_recv()

    sends = []
    for m in range(2):
        sends.append(kv_send(len(sends), m, me, 2, left))
        sends.append(kv_send(len(sends), m, me, 1, right))
    for m in range(2):
        sends.append(kv_send(len(sends), m, me, 0, pair))
    for c in sends:
        c.start()
    for i in range(QU_SLOTS):
        qu_copy(i).start()
    for i in range(KU_SLOTS):
        ku_copy(i).start()

    acc_q[...] = jnp.zeros_like(acc_q)

    def q_step(k, carry):
        for c in range(n_qd_c):
            qd_copy(k * n_qd_c + c).wait()
        for c in range(n_qd_c):
            cols = slice(c * COLS, (c + 1) * COLS)
            acc_q[:, cols] += jnp.dot(x_all[:, ds(k * ROWS, ROWS)], ring[k * n_qd_c + c], preferred_element_type=F32)
        return carry

    lax.fori_loop(0, n_down, q_step, 0)

    for m in range(2):
        rows = pl.ds(m * blk, blk)
        lat = acc_q[rows, :]
        inv = lax.rsqrt(jnp.mean(lat * lat, axis=-1, keepdims=True) + NORM_EPS)
        cq_all[my_rows(m, core), :] = (lat * inv * gain_q[...]).astype(BF16)
    cq_rc = [rcopy(cq_all.at[my_rows(m, core)], cq_all.at[my_rows(m, core)], cq_ss.at[m], cq_rs.at[m], pair) for m in range(2)]
    for c in cq_rc:
        c.start()

    second = []
    for m in range(2):
        kv_wait(m, left, 1)
        kv_wait(m, right, 2)
    second.append(kv_send(6, 0, left, 3, right))
    second.append(kv_send(7, 1, right, 3, left))
    for m in range(2):
        second.append(kv_send(8 + m, m, left, 4, pair))
        second.append(kv_send(10 + m, m, right, 5, pair))
    for c in second:
        c.start()
    sends += second
    for c in cq_rc:
        c.wait_recv()

    low = lane2 < ROPE_DIM

    def qu_step(i, carry):
        qu_copy(i).wait()
        f = jnp.dot(cq_all[...], qu[lax.rem(i, QU_SLOTS)], preferred_element_type=F32)
        for p in range(QU_HEADS // 2):
            base = 2 * QK_DIM * p
            t0 = f[:, base:base + LANES]
            t1 = f[:, base + LANES:base + 2 * LANES]
            t2 = f[:, base + 2 * LANES:base + 3 * LANES]
            q_s[i, :, base:base + LANES] = t0.astype(BF16)
            q_s[i, :, base + LANES:base + 2 * LANES] = pltpu.roll(jnp.where(low, t2, t1), ROPE_DIM, 1).astype(BF16)
            q_s[i, :, base + 2 * LANES:base + 3 * LANES] = rotate(jnp.where(low, t1, t2), trig[0], trig[1], first_half2).astype(BF16)

        @pl.when(i + QU_SLOTS < n_qu)
        def _():
            qu_copy(i + QU_SLOTS).start()

        return carry

    lax.fori_loop(0, n_qu // 2, qu_step, 0)
    third = []
    for m in range(2):
        kv_wait(m, opp, 3)
        third.append(kv_send(12 + m, m, opp, 6, pair))
    for c in third:
        c.start()
    sends += third
    lax.fori_loop(n_qu // 2, n_qu, qu_step, 0)
    n_early = RING - n_qd
    for g in range(n_early):
        wo_copy(g).start()

    other = 1 - 2 * core
    for m in range(2):
        kv_wait(m, pair, 0)
        kv_wait(m, left + other, 4)
        kv_wait(m, right + other, 5)
        kv_wait(m, opp + other, 6)
    lane3 = lax.broadcasted_iota(jnp.int32, (toks, LANES), 1)
    for m in range(2):
        t = kv_all[m, :, KV_LAT:].astype(F32)
        kr[0, m] = jnp.where(lane3 < ROPE_DIM, t, 0.0).astype(BF16)
        kr[1, m] = jnp.where(lane3 < ROPE_DIM, 0.0, t).astype(BF16)

    exp_scale = QK_DIM ** -0.5 * 1.4426950408889634
    kvs, s_scr, p_scr = (kvs0, kvs1), (s0, s1), (p0, p1)
    o_width = 2 * KU_HEADS * V_DIM

    def o_copy(t):
        cols = ds(core * (half_heads * V_DIM) + t * o_width, o_width)
        return rcopy(o_all.at[:, cols], o_all.at[:, cols], o_ss.at[t], o_rs.at[t], pair)

    def kv_up(b, i):
        for m in range(2):
            kvs[b][m] = jnp.dot(kv_all[m, :, :KV_LAT], ku[lax.rem(i, KU_SLOTS)], preferred_element_type=F32).astype(BF16)

    def scores(b, t):
        for m in range(2):
            rows = slice(m * q_rows, (m + 1) * q_rows)
            for j in range(KU_HEADS):
                base = 2 * QK_DIM * b
                nope = q_s[t, rows, base + LANES * j:base + LANES * (j + 1)]
                rope = q_s[t, rows, base + 2 * LANES:base + 3 * LANES]
                qc = jnp.concatenate([nope, rope], axis=1)
                kc = jnp.concatenate([kvs[b][m, :, KV_DIM * j:KV_DIM * j + NOPE_DIM], kr[j, m]], axis=1)
                s_scr[b][KU_HEADS * m + j] = lax.dot_general(qc, kc, (((1,), (1,)), ((), ())), preferred_element_type=F32)

    def softmax(b):
        step = 32
        for m in range(2):
            for j in range(KU_HEADS):
                for r in range(q_rows // step):
                    rows = slice(r * step, (r + 1) * step)
                    s = jnp.minimum(s_scr[b][KU_HEADS * m + j, rows, :], cap[m, rows, :])
                    top = jnp.max(s, axis=-1, keepdims=True)
                    e = jnp.exp2((s - top) * exp_scale)
                    inv = 1.0 / jnp.sum(e, axis=-1, keepdims=True)
                    p_scr[b][KU_HEADS * m + j, rows, :] = (e * inv).astype(BF16)

    def values(b, t):
        for m in range(2):
            rows = slice(m * q_rows, (m + 1) * q_rows)
            for j in range(KU_HEADS):
                v = kvs[b][m, :, KV_DIM * j + NOPE_DIM:KV_DIM * (j + 1)]
                o = jnp.dot(p_scr[b][KU_HEADS * m + j], v, preferred_element_type=F32).astype(BF16)
                col = pl.multiple_of(core * (half_heads * V_DIM) + t * o_width + (KU_HEADS * b + j) * V_DIM, V_DIM)
                o_all[rows, pl.ds(col, V_DIM)] = o

    ku_copy(0).wait()
    kv_up(0, 0)
    scores(0, 0)
    ku_copy(KU_SLOTS).start()
    n_loop = n_ku // 2 - 1
    n_late = RING - n_early
    per = -(-n_late // n_loop)

    def at_step(t, carry):
        ku_copy(2 * t + 1).wait()
        ku_copy(2 * t + 2).wait()
        softmax(0)
        kv_up(1, 2 * t + 1)
        values(0, t)
        scores(1, t)
        softmax(1)
        kv_up(0, 2 * t + 2)
        values(1, t)
        scores(0, t + 1)
        for d in (5, 6):
            @pl.when(2 * t + d < n_ku)
            def _():
                ku_copy(2 * t + d).start()
        for d in range(per):
            g = n_early + t * per + d

            @pl.when(g < RING)
            def _():
                wo_copy(g).start()

        o_copy(t).start()
        return carry

    lax.fori_loop(0, n_loop, at_step, 0)
    last = n_loop
    ku_copy(n_ku - 1).wait()
    softmax(0)
    kv_up(1, n_ku - 1)
    values(0, last)
    scores(1, last)
    softmax(1)
    values(1, last)
    o_copy(last).start()

    for t in range(n_loop + 1):
        cols = ds((1 - core) * (half_heads * V_DIM) + t * o_width, o_width)
        rcopy(o_all.at[:, cols], o_all.at[:, cols], o_ss.at[t], o_rs.at[t], pair).wait_recv()

    y_out = (y_one, y_two)

    def y_copies(n):
        slot = lax.rem(n, 2)
        cols = ds(core * y_cols + n * COLS, COLS)
        local = [pltpu.make_async_copy(y_st.at[slot, my_rows(m, core)], y_out[m].at[:, cols], y_ls.at[slot, m]) for m in range(2)]
        remote = [rcopy(y_st.at[slot, my_rows(m, 1 - core)], y_out[m].at[:, cols], y_ss.at[slot, m], y_rs.at[n, m], pair) for m in range(2)]
        return local, remote

    def y_wait(n):
        local, remote = y_copies(n)
        for m in range(2):
            local[m].wait()
            remote[m].wait_send()

    def wo_step(n, carry):
        for k in range(n_wo_k):
            g = n * n_wo_k + k
            wo_copy(g).wait()
            d = jnp.dot(o_all[:, k * ROWS:(k + 1) * ROWS], ring[wo_slot(g)], preferred_element_type=F32)
            if k == 0:
                acc_y[...] = d
            else:
                acc_y[...] += d

            @pl.when(g + RING < n_wo)
            def _():
                wo_copy(g + RING).start()

        @pl.when(n >= 2)
        def _():
            y_wait(n - 2)

        y_st[lax.rem(n, 2)] = acc_y[...].astype(BF16)
        local, remote = y_copies(n)
        for m in range(2):
            local[m].start()
            remote[m].start()
        return carry

    lax.fori_loop(0, n_wo_n, wo_step, 0)
    y_wait(n_wo_n - 2)
    y_wait(n_wo_n - 1)
    for n in range(n_wo_n):
        cols = ds((1 - core) * y_cols + n * COLS, COLS)
        for m in range(2):
            rcopy(y_st.at[0, my_rows(m, core)], y_out[m].at[:, cols], y_ss.at[0, m], y_rs.at[n, m], pair).wait_recv()
    for m in range(2):
        pos_rc[m].wait_send()
        cq_rc[m].wait_send()
    for c in sends:
        c.wait_send()
    for t in range(n_loop + 1):
        o_copy(t).wait_send()


def mla(n_sp, x_one, x_two, pos, freq, w_qd, gain_q, w_qu, w_kvd, gain_kv, w_kvu, w_out):
    blk, d_model = x_one.shape
    heads = w_out.shape[0] // V_DIM
    toks = n_sp * blk
    q_rows = 2 * blk
    n_down = d_model // ROWS
    n_qu = heads // 2 // QU_HEADS
    n_ku = heads // 2 // KU_HEADS
    n_wo_n = d_model // 2 // COLS
    hbm = pl.BlockSpec(memory_space=pl.ANY)
    vmem = pl.BlockSpec(memory_space=pltpu.VMEM)
    dma = pltpu.SemaphoreType.DMA
    units = 2 * KU_HEADS
    return pl.pallas_call(
        functools.partial(body, n_sp, heads, d_model, blk),
        out_shape=[jax.ShapeDtypeStruct((blk, d_model), BF16)] * 2,
        in_specs=[hbm, hbm, hbm, vmem, hbm, vmem, hbm, hbm, vmem, hbm, hbm],
        out_specs=[hbm, hbm],
        scratch_shapes=[
            pltpu.VMEM((2 * blk, d_model), BF16),
            pltpu.VMEM((2 * q_rows, LANES), F32),
            pltpu.VMEM((2, 2 * q_rows, LANES), F32),
            pltpu.VMEM((n_down, KV_LAT + ROPE_DIM, ROWS), BF16),
            pltpu.VMEM((RING, ROWS, COLS), BF16),
            pltpu.VMEM((QU_SLOTS, Q_LAT, QU_HEADS * QK_DIM), BF16),
            pltpu.VMEM((KU_SLOTS, KV_LAT, KU_HEADS * KV_DIM), BF16),
            pltpu.VMEM((2 * blk, KV_LAT + ROPE_DIM), F32),
            pltpu.VMEM((2 * blk, Q_LAT), F32),
            pltpu.VMEM((2, toks, KVW), BF16),
            pltpu.VMEM((2 * q_rows, Q_LAT), BF16),
            pltpu.VMEM((2, q_rows, toks), F32),
            pltpu.VMEM((2, 2, toks, LANES), BF16),
            pltpu.VMEM((n_qu, 2 * q_rows, QU_HEADS * QK_DIM), BF16),
            pltpu.VMEM((2, toks, KU_HEADS * KV_DIM), BF16),
            pltpu.VMEM((2, toks, KU_HEADS * KV_DIM), BF16),
            pltpu.VMEM((units, q_rows, toks), F32),
            pltpu.VMEM((units, q_rows, toks), F32),
            pltpu.VMEM((units, q_rows, toks), BF16),
            pltpu.VMEM((units, q_rows, toks), BF16),
            pltpu.VMEM((2 * q_rows, heads * V_DIM), BF16),
            pltpu.VMEM((2 * q_rows, COLS), F32),
            pltpu.VMEM((2, 2 * q_rows, COLS), BF16),
            dma((2,)), dma((2,)), dma((2,)), dma((2,)),
            dma((n_down,)), dma((RING,)), dma((QU_SLOTS,)), dma((KU_SLOTS,)),
            dma((14,)), dma((7, 2)),
            dma((2,)), dma((2,)),
            dma((n_ku // 2,)), dma((n_ku // 2,)),
            dma((2, 2)), dma((2, 2)), dma((n_wo_n, 2)),
        ],
        compiler_params=pltpu.CompilerParams(
            collective_id=0, has_side_effects=True, vmem_limit_bytes=67043328),
        name="mla",
    )(x_one, x_two, pos, freq, w_qd, gain_q, w_qu, w_kvd, gain_kv, w_kvu, w_out)


def solution(mesh):
    tok_spec = P(('dp', 'sp'), None)
    idx_spec = P(('dp', 'sp'))
    n_sp = mesh.shape['sp']
    freq = ROPE_BASE ** (-(np.arange(LANES) % HALF_ROPE).astype(np.float64) / HALF_ROPE)
    freq = freq.astype(np.float32)[None, :]

    def local_body(x_one, seg_one, pos_one, x_two, seg_two, pos_two, w_qdown, gain_q, w_qup, w_kvdown, gain_kv, w_kvup, w_out):
        pos = jnp.concatenate([pos_one, pos_two]).astype(F32)
        pos = jnp.broadcast_to(pos[:, None], (pos.shape[0], LANES))
        return mla(n_sp, x_one, x_two, pos, jnp.asarray(freq), w_qdown, gain_q.astype(F32)[None, :], w_qup, w_kvdown.T, gain_kv.astype(F32)[None, :], w_kvup, w_out)

    return jax.shard_map(local_body, mesh=mesh, in_specs=(tok_spec, idx_spec, idx_spec, tok_spec, idx_spec, idx_spec) + (P(),) * 7, out_specs=(tok_spec, tok_spec), check_vma=False)
```

time: 108 us -> 84.1 us (0.78)
  local copies, waits for them, and re-layouts: 19.7 us -> 6.32 us
  Pallas kernels: 85.6 us -> 74.8 us
    unnamed x3 -> x2, local copies, waits for them, and re-layouts: 16.7 us -> 4.32 us
    pallas_call x1, Pallas kernels: 85.6 us -> 74.8 us  [mla(): pl.pallas_call(functools.partial(body, n_sp, heads, d_model, blk), out_sh...]
    reshape x2 -> x0, local copies, waits for them, and re-layouts: 2.55 us -> none  [the longest x1 1.28 us: local_body(): gain_q.reshape(1, -1)]
    broadcast_in_dim x2, local copies, waits for them, and re-layouts: 0.14 us -> 1.99 us  [the longest x1 1.28 us: local_body(): gain_q.astype(F32)[None, :]]
    broadcast_in_dim x0 -> x1, other arithmetic: none -> 1.27 us  [local_body(): gain_kv.astype(F32)[None, :]]
where the time goes in v1:
time: 84.1 us; the launch traced here: 83.8 us
  Pallas kernels  74.8 us (89%)
  local copies, waits for them, and re-layouts  6.32 us (8%)
  other arithmetic  2.01 us (2%)
    pallas_call x1, Pallas kernels, mla(): pl.pallas_call(functools.partial(body, n_sp, heads, d_model, blk), out_sh...  74.8 us
    unnamed x2, local copies, waits for them, and re-layouts  4.32 us

profile of v1, /device:TPU:81, one launch (start us, length us, event | category | flops | bytes accessed | tf_op | source)
XLA Modules:
  0.0 83.8 jit_solution(13268390186802944925)
XLA Ops:
  0.6 0.7 add_convert_fusion
  1.4 1.3 %broadcast_in_dim.22 = f32[512]{0:T(512)} convert(bf16[512]{0:T(512)(128)(2,1)} %param.22) | non-fusion elementwise | flops 512 | bytes 3072 | tf_op jit(solution)/shard_map/broadcast_in_dim | solution.py:483
  2.6 1.3 %reshape.19.gain_q = f32[1,1536]{1,0:T(1,128)} reshape(bf16[1536]{0:T(1024)(128)(2,1)} %param.19) | data formatting | bytes 9216 | tf_op jit(solution)/shard_map/broadcast_in_dim | solution.py:483
  3.9 0.7 broadcast_in_dim.16.pos
  4.6 74.8 %mla.1 = (bf16[64,7168]{1,0:T(8,128)(2,1)}, bf16[64,7168]{1,0:T(8,128)(2,1)}) custom-call(bf16[64,7168]{1,0:T(8,128)(2,1)} %x_one.1, bf16[64,7168]{1,0:T(8,128)(2,1)} %x_two.1, f32[128,128]{1,0:T(8,128)} %broadcast_in_dim.16.pos, f32[1,128]{1,0:T(1,128)} %constant.2.clone.freq, bf16[7168,1536]{1,0:T(8,128)(2,1)} %w_qd.1, f32[1,1536]{1,0:T(1,128)} %reshape.19.gain_q, ...), custom_call_target="tpu_custom_call" | custom-call | tf_op jit(solution)/shard_map/mla/pallas_call | solution.py:431
  79.4 2.2 %copy.16 = bf16[64,7168]{1,0:T(8,128)(2,1)} copy(bf16[64,7168]{1,0:T(8,128)(2,1)} %get-tuple-element.4) | data formatting | bytes 1835008
  81.6 2.2 %copy.17 = bf16[64,7168]{1,0:T(8,128)(2,1)} copy(bf16[64,7168]{1,0:T(8,128)(2,1)} %get-tuple-element.5) | data formatting | bytes 1835008

commit v2 on v1

--- a/solution.py
+++ b/solution.py
@@ -22,9 +22,10 @@
 
 ROWS = 1024
 COLS = 512
-RING = 26
+RING = 25
+WO_RING = 24
 QU_HEADS = 4
-QU_SLOTS = 2
+QU_SLOTS = 3
 KU_HEADS = 2
 KU_SLOTS = 4
 KVW = KV_LAT + LANES
@@ -35,11 +36,11 @@
 
 
 def body(n_sp, heads, d_model, blk,
-         x_one, x_two, pos, freq, w_qd, gain_q, w_qu, w_kvd, gain_kv, w_kvu, w_out,
+         x_one, x_two, pos_one, pos_two, freq, w_qd, gain_q, w_qu, w_kvd, gain_kv, w_kvu, w_out,
          y_one, y_two,
-         x_all, pos_all, trig, kvd, ring, qu, ku, acc_kv, acc_q, kv_all, cq_all,
+         x_all, pos_s, ends, pos_all, trig, ring, qu, ku, acc_kv, acc_q, kv_all, cq_all,
          cap, kr, q_s, kvs0, kvs1, s0, s1, p0, p1, o_all, acc_y, y_st,
-         x_sem, pos_sem, pos_ss, pos_rs, kvd_sem, ring_sem, qu_sem, ku_sem,
+         x_sem, x_ss, x_rs, pos_sem, pos_ss, pos_rs, ring_sem, qd_sem, qu_sem, ku_sem,
          kv_ss, kv_rs, cq_ss, cq_rs, o_ss, o_rs, y_ls, y_ss, y_rs):
     me = lax.axis_index("sp")
     core = lax.rem(me, 2)
@@ -53,8 +54,8 @@
     half_heads = heads // 2
     y_cols = d_model // 2
     n_down = d_model // ROWS
-    n_qd_c = Q_LAT // COLS
-    n_qd = n_down * n_qd_c
+    q_cols = Q_LAT // 2
+    n_kvd = d_model // COLS
     n_qu = half_heads // QU_HEADS
     n_ku = half_heads // KU_HEADS
     n_wo_k = heads * V_DIM // ROWS
@@ -70,11 +71,20 @@
         return pl.ds(start if isinstance(start, int) else pl.multiple_of(start, size), size)
 
     def kvd_copy(k):
-        return pltpu.make_async_copy(w_kvd.at[:, ds(k * ROWS, ROWS)], kvd.at[k], kvd_sem.at[k])
-
-    def qd_copy(g):
-        src = w_qd.at[ds(g // n_qd_c * ROWS, ROWS), ds(lax.rem(g, n_qd_c) * COLS, COLS)]
-        return pltpu.make_async_copy(src, ring.at[g], ring_sem.at[g])
+        dst = ring.at[k, pl.ds(0, KV_LAT + ROPE_DIM)]
+        return pltpu.make_async_copy(w_kvd.at[:, ds(k * COLS, COLS)], dst, ring_sem.at[k])
+
+    half = COLS // 2
+
+    def qd_refs(k):
+        return ring.at[n_kvd + k], ring.at[n_kvd + n_down + k // 2, :, ds(lax.rem(k, 2) * half, half)]
+
+    def qd_copies(k):
+        col = core * q_cols
+        rows = ds(k * ROWS, ROWS)
+        one, two = qd_refs(k)
+        return (pltpu.make_async_copy(w_qd.at[rows, pl.ds(pl.multiple_of(col, half), COLS)], one, qd_sem.at[k, 0]),
+                pltpu.make_async_copy(w_qd.at[rows, pl.ds(pl.multiple_of(col + COLS, half), half)], two, qd_sem.at[k, 1]))
 
     def qu_copy(i):
         width = QU_HEADS * QK_DIM
@@ -88,46 +98,135 @@
         slot = lax.rem(i, KU_SLOTS)
         return pltpu.make_async_copy(w_kvu.at[:, cols], ku.at[slot], ku_sem.at[slot])
 
-    def wo_slot(g):
-        return lax.rem(g + n_qd, RING)
-
     def wo_copy(g):
         rows = ds(lax.rem(g, n_wo_k) * ROWS, ROWS)
         cols = ds(core * y_cols + g // n_wo_k * COLS, COLS)
-        return pltpu.make_async_copy(w_out.at[rows, cols], ring.at[wo_slot(g)], ring_sem.at[wo_slot(g)])
+        slot = lax.rem(g, WO_RING)
+        return pltpu.make_async_copy(w_out.at[rows, cols], ring.at[slot], ring_sem.at[slot])
 
     x_in = (x_one, x_two)
-    x_cp = [pltpu.make_async_copy(x_in[m], x_all.at[pl.ds(m * blk, blk)], x_sem.at[m]) for m in range(2)]
-    for c in x_cp:
+
+    def x_rows(m, c):
+        return ds(c * q_rows + m * blk, blk)
+
+    def my_rows(m, c):
+        return ds(m * q_rows + c * blk, blk)
+
+    pos_cp = [pltpu.make_async_copy((pos_one, pos_two)[m], pos_s.at[m], pos_sem.at[m]) for m in range(2)]
+    x_cp = [pltpu.make_async_copy(x_in[m], x_all.at[x_rows(m, core)], x_sem.at[m]) for m in range(2)]
+    for c in pos_cp + x_cp:
         c.start()
-    for k in range(n_down):
+    for k in range(n_kvd):
         kvd_copy(k).start()
-    for g in range(n_qd):
-        qd_copy(g).start()
 
     barrier = pltpu.get_barrier_semaphore()
     for dev in (pair, left, right):
         pl.semaphore_signal(barrier, inc=1, device_id={"sp": dev}, device_id_type=pl.DeviceIdType.MESH)
+    for c in pos_cp:
+        c.wait()
+    for m in range(2):
+        first, final = pos_s[m, 0], pos_s[m, blk - 1]
+        ends[core, 2 * m] = jnp.full((8, LANES), first, jnp.int32).astype(F32)
+        ends[core, 2 * m + 1] = jnp.full((8, LANES), final, jnp.int32).astype(F32)
+
+    lane = lax.broadcasted_iota(jnp.int32, (blk, LANES), 1)
+    first_half = lax.rem(lane, ROPE_DIM) < HALF_ROPE
+
+    def positions(m, c):
+        tok = lax.broadcasted_iota(jnp.int32, (blk, LANES), 0).astype(F32)
+        first = jnp.concatenate([ends[c, 2 * m]] * (blk // 8), axis=0)
+        back = jnp.concatenate([ends[c, 2 * m + 1]] * (blk // 8), axis=0) - (blk - 1)
+        val = jnp.where(tok + back >= 0, tok + back, tok + first)
+        rows = my_rows(m, c)
+        pos_all[rows, :] = val
+        ang = val * freq[...]
+        sin = jnp.sin(ang)
+        trig[0, rows, :] = jnp.cos(ang)
+        trig[1, rows, :] = jnp.where(first_half, -sin, sin)
+
+    for m in range(2):
+        positions(m, core)
     pl.semaphore_wait(barrier, 3)
-
-    def my_rows(m, c):
-        return ds(m * q_rows + c * blk, blk)
-
-    pos_cp = [pltpu.make_async_copy(pos.at[pl.ds(m * blk, blk)], pos_all.at[my_rows(m, core)], pos_sem.at[m]) for m in range(2)]
-    pos_rc = [rcopy(pos.at[pl.ds(m * blk, blk)], pos_all.at[my_rows(m, core)], pos_ss.at[m], pos_rs.at[m], pair) for m in range(2)]
-    for m in range(2):
-        pos_cp[m].start()
-        pos_rc[m].start()
-
-    for m in range(2):
-        pos_cp[m].wait()
-        pos_rc[m].wait_recv()
-    lane2 = lax.broadcasted_iota(jnp.int32, (2 * q_rows, LANES), 1)
-    first_half2 = lax.rem(lane2, ROPE_DIM) < HALF_ROPE
-    ang = pos_all[...] * freq[...]
-    trig[0] = jnp.cos(ang)
-    sin = jnp.sin(ang)
-    trig[1] = jnp.where(first_half2, -sin, sin)
+    x_rc = [rcopy(x_in[m], x_all.at[x_rows(m, core)], x_ss.at[m], x_rs.at[m], pair) for m in range(2)]
+    for c in x_rc:
+        c.start()
+    ends_rc = rcopy(ends.at[core], ends.at[core], pos_ss.at[0], pos_rs.at[0], pair)
+    for c in x_cp:
+        c.wait()
+
+    acc_kv[...] = jnp.zeros_like(acc_kv)
+
+    my_x = ds(core * q_rows, q_rows)
+
+    def kv_step(k, carry):
+        for c in qd_copies(k):
+            c.start()
+        for c in range(2):
+            kvd_copy(2 * k + c).wait()
+        x_k = x_all[my_x, ds(k * ROWS, ROWS)]
+        w_k = jnp.concatenate([ring[2 * k, :KV_LAT + ROPE_DIM], ring[2 * k + 1, :KV_LAT + ROPE_DIM]], axis=1)
+        acc_kv[...] += lax.dot_general(x_k, w_k, (((1,), (1,)), ((), ())), preferred_element_type=F32)
+        return carry
+
+    lax.fori_loop(0, n_down, kv_step, 0)
+    ends_rc.start()
+
+    def rotate(z, cos, sin, sel):
+        swapped = jnp.where(sel, pltpu.roll(z, LANES - HALF_ROPE, 1), pltpu.roll(z, HALF_ROPE, 1))
+        return z * cos + swapped * sin
+
+    own = ds(me * blk, blk)
+    for m in range(2):
+        rows = pl.ds(m * blk, blk)
+        lat = acc_kv[rows, :KV_LAT]
+        inv = lax.rsqrt(jnp.mean(lat * lat, axis=-1, keepdims=True) + NORM_EPS)
+        kv_all[m, own, :KV_LAT] = (lat * inv * gain_kv[...].astype(F32).reshape(1, -1)).astype(BF16)
+        raw = acc_kv[rows, KV_LAT:]
+        raw = jnp.concatenate([raw, raw], axis=1)
+        kv_all[m, own, KV_LAT:] = rotate(raw, trig[0, my_rows(m, core), :], trig[1, my_rows(m, core), :], first_half).astype(BF16)
+
+    def piece(m, dev):
+        return kv_all.at[m, ds(dev * blk, blk)]
+
+    def kv_send(i, m, src_dev, role, dev):
+        return rcopy(piece(m, src_dev), piece(m, src_dev), kv_ss.at[i], kv_rs.at[role, m], dev)
+
+    def kv_wait(m, src_dev, role):
+        rcopy(piece(m, src_dev), piece(m, src_dev), kv_ss.at[0], kv_rs.at[role, m], pair).wait_recv()
+
+    sends = []
+    for m in range(2):
+        sends.append(kv_send(len(sends), m, me, 2, left))
+        sends.append(kv_send(len(sends), m, me, 1, right))
+    for m in range(2):
+        sends.append(kv_send(len(sends), m, me, 0, pair))
+    for c in sends:
+        c.start()
+    for i in range(QU_SLOTS):
+        qu_copy(i).start(priority=1)
+    for i in range(KU_SLOTS):
+        ku_copy(i).start(priority=1)
+
+    for c in x_rc:
+        c.wait_recv()
+    my_cols = ds(core * q_cols, q_cols)
+    acc_q[:, my_cols] = jnp.zeros((2 * q_rows, q_cols), F32)
+
+    def q_step(k, carry):
+        for c in qd_copies(k):
+            c.wait()
+        one, two = qd_refs(k)
+        w_k = jnp.concatenate([one[...], two[...]], axis=1)
+        acc_q[:, my_cols] += jnp.dot(x_all[:, ds(k * ROWS, ROWS)], w_k, preferred_element_type=F32)
+        return carry
+
+    lax.fori_loop(0, n_down, q_step, 0)
+    cq_rc = rcopy(acc_q.at[:, my_cols], acc_q.at[:, my_cols], cq_ss.at[0], cq_rs.at[0], pair)
+    cq_rc.start()
+
+    ends_rc.wait_recv()
+    for m in range(2):
+        positions(m, 1 - core)
     for m in range(2):
         row = lax.broadcasted_iota(jnp.int32, (q_rows, LANES), 0) + chip * q_rows
         start = row.astype(F32) - pos_all[m * q_rows:(m + 1) * q_rows, :]
@@ -135,77 +234,13 @@
             key = lax.broadcasted_iota(jnp.int32, (q_rows, LANES), 1) + c * LANES
             keep = (key <= row) & (key.astype(F32) >= start)
             cap[m, :, c * LANES:(c + 1) * LANES] = jnp.where(keep, BIG, MASKED)
-    for c in x_cp:
-        c.wait()
-
-    acc_kv[...] = jnp.zeros_like(acc_kv)
-
-    def kv_step(k, carry):
-        kvd_copy(k).wait()
-        acc_kv[...] += lax.dot_general(x_all[:, ds(k * ROWS, ROWS)], kvd[k], (((1,), (1,)), ((), ())), preferred_element_type=F32)
-        return carry
-
-    lax.fori_loop(0, n_down, kv_step, 0)
-
-    lane = lax.broadcasted_iota(jnp.int32, (blk, LANES), 1)
-    first_half = lax.rem(lane, ROPE_DIM) < HALF_ROPE
-
-    def rotate(z, cos, sin, sel):
-        swapped = jnp.where(sel, pltpu.roll(z, LANES - HALF_ROPE, 1), pltpu.roll(z, HALF_ROPE, 1))
-        return z * cos + swapped * sin
-
-    own = ds(me * blk, blk)
-    for m in range(2):
-        rows = pl.ds(m * blk, blk)
-        lat = acc_kv[rows, :KV_LAT]
-        inv = lax.rsqrt(jnp.mean(lat * lat, axis=-1, keepdims=True) + NORM_EPS)
-        kv_all[m, own, :KV_LAT] = (lat * inv * gain_kv[...]).astype(BF16)
-        raw = acc_kv[rows, KV_LAT:]
-        raw = jnp.concatenate([raw, raw], axis=1)
-        kv_all[m, own, KV_LAT:] = rotate(raw, trig[0, my_rows(m, core), :], trig[1, my_rows(m, core), :], first_half).astype(BF16)
-
-    def piece(m, dev):
-        return kv_all.at[m, ds(dev * blk, blk)]
-
-    def kv_send(i, m, src_dev, role, dev):
-        return rcopy(piece(m, src_dev), piece(m, src_dev), kv_ss.at[i], kv_rs.at[role, m], dev)
-
-    def kv_wait(m, src_dev, role):
-        rcopy(piece(m, src_dev), piece(m, src_dev), kv_ss.at[0], kv_rs.at[role, m], pair).wait_recv()
-
-    sends = []
-    for m in range(2):
-        sends.append(kv_send(len(sends), m, me, 2, left))
-        sends.append(kv_send(len(sends), m, me, 1, right))
-    for m in range(2):
-        sends.append(kv_send(len(sends), m, me, 0, pair))
-    for c in sends:
-        c.start()
-    for i in range(QU_SLOTS):
-        qu_copy(i).start()
-    for i in range(KU_SLOTS):
-        ku_copy(i).start()
-
-    acc_q[...] = jnp.zeros_like(acc_q)
-
-    def q_step(k, carry):
-        for c in range(n_qd_c):
-            qd_copy(k * n_qd_c + c).wait()
-        for c in range(n_qd_c):
-            cols = slice(c * COLS, (c + 1) * COLS)
-            acc_q[:, cols] += jnp.dot(x_all[:, ds(k * ROWS, ROWS)], ring[k * n_qd_c + c], preferred_element_type=F32)
-        return carry
-
-    lax.fori_loop(0, n_down, q_step, 0)
-
-    for m in range(2):
-        rows = pl.ds(m * blk, blk)
-        lat = acc_q[rows, :]
-        inv = lax.rsqrt(jnp.mean(lat * lat, axis=-1, keepdims=True) + NORM_EPS)
-        cq_all[my_rows(m, core), :] = (lat * inv * gain_q[...]).astype(BF16)
-    cq_rc = [rcopy(cq_all.at[my_rows(m, core)], cq_all.at[my_rows(m, core)], cq_ss.at[m], cq_rs.at[m], pair) for m in range(2)]
-    for c in cq_rc:
-        c.start()
+
+    cq_rc.wait_recv()
+    for m in range(2):
+        for c in range(2):
+            lat = acc_q[c * q_rows + m * blk:c * q_rows + (m + 1) * blk, :]
+            inv = lax.rsqrt(jnp.mean(lat * lat, axis=-1, keepdims=True) + NORM_EPS)
+            cq_all[my_rows(m, c), :] = (lat * inv * gain_q[...].astype(F32).reshape(1, -1)).astype(BF16)
 
     second = []
     for m in range(2):
@@ -219,9 +254,9 @@
     for c in second:
         c.start()
     sends += second
-    for c in cq_rc:
-        c.wait_recv()
-
+
+    lane2 = lax.broadcasted_iota(jnp.int32, (2 * q_rows, LANES), 1)
+    first_half2 = lax.rem(lane2, ROPE_DIM) < HALF_ROPE
     low = lane2 < ROPE_DIM
 
     def qu_step(i, carry):
@@ -242,7 +277,8 @@
 
         return carry
 
-    lax.fori_loop(0, n_qu // 2, qu_step, 0)
+    n_before = n_qu * 3 // 4
+    lax.fori_loop(0, n_before, qu_step, 0)
     third = []
     for m in range(2):
         kv_wait(m, opp, 3)
@@ -250,10 +286,10 @@
     for c in third:
         c.start()
     sends += third
-    lax.fori_loop(n_qu // 2, n_qu, qu_step, 0)
-    n_early = RING - n_qd
+    lax.fori_loop(n_before, n_qu, qu_step, 0)
+    n_early = n_wo_k
     for g in range(n_early):
-        wo_copy(g).start()
+        wo_copy(g).start(priority=1)
 
     other = 1 - 2 * core
     for m in range(2):
@@ -316,7 +352,7 @@
     scores(0, 0)
     ku_copy(KU_SLOTS).start()
     n_loop = n_ku // 2 - 1
-    n_late = RING - n_early
+    n_late = WO_RING - n_early
     per = -(-n_late // n_loop)
 
     def at_step(t, carry):
@@ -337,9 +373,9 @@
         for d in range(per):
             g = n_early + t * per + d
 
-            @pl.when(g < RING)
+            @pl.when(g < WO_RING)
             def _():
-                wo_copy(g).start()
+                wo_copy(g).start(priority=1)
 
         o_copy(t).start()
         return carry
@@ -376,17 +412,15 @@
 
     def wo_step(n, carry):
         for k in range(n_wo_k):
-            g = n * n_wo_k + k
-            wo_copy(g).wait()
-            d = jnp.dot(o_all[:, k * ROWS:(k + 1) * ROWS], ring[wo_slot(g)], preferred_element_type=F32)
-            if k == 0:
-                acc_y[...] = d
-            else:
-                acc_y[...] += d
-
-            @pl.when(g + RING < n_wo)
-            def _():
-                wo_copy(g + RING).start()
+            wo_copy(n * n_wo_k + k).wait()
+        first = lax.rem(n * n_wo_k, WO_RING)
+        w_n = ring[pl.ds(first, n_wo_k)].reshape(n_wo_k * ROWS, COLS)
+        acc_y[...] = jnp.dot(o_all[...], w_n, preferred_element_type=F32)
+
+        @pl.when((n + 1) * n_wo_k + WO_RING <= n_wo)
+        def _():
+            for k in range(n_wo_k):
+                wo_copy(n * n_wo_k + WO_RING + k).start()
 
         @pl.when(n >= 2)
         def _():
@@ -406,16 +440,15 @@
         cols = ds((1 - core) * y_cols + n * COLS, COLS)
         for m in range(2):
             rcopy(y_st.at[0, my_rows(m, core)], y_out[m].at[:, cols], y_ss.at[0, m], y_rs.at[n, m], pair).wait_recv()
-    for m in range(2):
-        pos_rc[m].wait_send()
-        cq_rc[m].wait_send()
+    for c in x_rc + [ends_rc, cq_rc]:
+        c.wait_send()
     for c in sends:
         c.wait_send()
     for t in range(n_loop + 1):
         o_copy(t).wait_send()
 
 
-def mla(n_sp, x_one, x_two, pos, freq, w_qd, gain_q, w_qu, w_kvd, gain_kv, w_kvu, w_out):
+def mla(n_sp, x_one, x_two, pos_one, pos_two, freq, w_qd, gain_q, w_qu, w_kvd, gain_kv, w_kvu, w_out):
     blk, d_model = x_one.shape
     heads = w_out.shape[0] // V_DIM
     toks = n_sp * blk
@@ -431,18 +464,19 @@
     return pl.pallas_call(
         functools.partial(body, n_sp, heads, d_model, blk),
         out_shape=[jax.ShapeDtypeStruct((blk, d_model), BF16)] * 2,
-        in_specs=[hbm, hbm, hbm, vmem, hbm, vmem, hbm, hbm, vmem, hbm, hbm],
+        in_specs=[hbm, hbm, hbm, hbm, vmem, hbm, vmem, hbm, hbm, vmem, hbm, hbm],
         out_specs=[hbm, hbm],
         scratch_shapes=[
-            pltpu.VMEM((2 * blk, d_model), BF16),
+            pltpu.VMEM((2 * q_rows, d_model), BF16),
+            pltpu.SMEM((2, blk), jnp.int32),
+            pltpu.VMEM((2, 4, 8, LANES), F32),
             pltpu.VMEM((2 * q_rows, LANES), F32),
             pltpu.VMEM((2, 2 * q_rows, LANES), F32),
-            pltpu.VMEM((n_down, KV_LAT + ROPE_DIM, ROWS), BF16),
             pltpu.VMEM((RING, ROWS, COLS), BF16),
             pltpu.VMEM((QU_SLOTS, Q_LAT, QU_HEADS * QK_DIM), BF16),
             pltpu.VMEM((KU_SLOTS, KV_LAT, KU_HEADS * KV_DIM), BF16),
             pltpu.VMEM((2 * blk, KV_LAT + ROPE_DIM), F32),
-            pltpu.VMEM((2 * blk, Q_LAT), F32),
+            pltpu.VMEM((2 * q_rows, Q_LAT), F32),
             pltpu.VMEM((2, toks, KVW), BF16),
             pltpu.VMEM((2 * q_rows, Q_LAT), BF16),
             pltpu.VMEM((2, q_rows, toks), F32),
@@ -457,17 +491,17 @@
             pltpu.VMEM((2 * q_rows, heads * V_DIM), BF16),
             pltpu.VMEM((2 * q_rows, COLS), F32),
             pltpu.VMEM((2, 2 * q_rows, COLS), BF16),
-            dma((2,)), dma((2,)), dma((2,)), dma((2,)),
-            dma((n_down,)), dma((RING,)), dma((QU_SLOTS,)), dma((KU_SLOTS,)),
+            dma((2,)), dma((2,)), dma((2,)), dma((2,)), dma((1,)), dma((1,)),
+            dma((RING,)), dma((n_down, 2)), dma((QU_SLOTS,)), dma((KU_SLOTS,)),
             dma((14,)), dma((7, 2)),
-            dma((2,)), dma((2,)),
+            dma((1,)), dma((1,)),
             dma((n_ku // 2,)), dma((n_ku // 2,)),
             dma((2, 2)), dma((2, 2)), dma((n_wo_n, 2)),
         ],
         compiler_params=pltpu.CompilerParams(
             collective_id=0, has_side_effects=True, vmem_limit_bytes=67043328),
         name="mla",
-    )(x_one, x_two, pos, freq, w_qd, gain_q, w_qu, w_kvd, gain_kv, w_kvu, w_out)
+    )(x_one, x_two, pos_one, pos_two, freq, w_qd, gain_q, w_qu, w_kvd, gain_kv, w_kvu, w_out)
 
 
 def solution(mesh):
@@ -478,8 +512,6 @@
     freq = freq.astype(np.float32)[None, :]
 
     def local_body(x_one, seg_one, pos_one, x_two, seg_two, pos_two, w_qdown, gain_q, w_qup, w_kvdown, gain_kv, w_kvup, w_out):
-        pos = jnp.concatenate([pos_one, pos_two]).astype(F32)
-        pos = jnp.broadcast_to(pos[:, None], (pos.shape[0], LANES))
-        return mla(n_sp, x_one, x_two, pos, jnp.asarray(freq), w_qdown, gain_q.astype(F32)[None, :], w_qup, w_kvdown.T, gain_kv.astype(F32)[None, :], w_kvup, w_out)
+        return mla(n_sp, x_one, x_two, pos_one, pos_two, jnp.asarray(freq), w_qdown, gain_q, w_qup, w_kvdown.T, gain_kv, w_kvup, w_out)
 
     return jax.shard_map(local_body, mesh=mesh, in_specs=(tok_spec, idx_spec, idx_spec, tok_spec, idx_spec, idx_spec) + (P(),) * 7, out_specs=(tok_spec, tok_spec), check_vma=False)

time: 84.1 us -> 69.9 us (0.83)
  Pallas kernels: 74.8 us -> 64.7 us
  other arithmetic: 2.01 us -> 0 us
  local copies, waits for them, and re-layouts: 6.32 us -> 4.32 us
    pallas_call x1, Pallas kernels: 74.8 us -> 64.7 us  [mla(): pl.pallas_call(functools.partial(body, n_sp, heads, d_model, blk), out_sh...]
    broadcast_in_dim x2 -> x0, local copies, waits for them, and re-layouts: 1.99 us -> none  [the longest x1 1.28 us: local_body(): gain_q.astype(F32)[None, :]]
    broadcast_in_dim x1 -> x0, other arithmetic: 1.27 us -> none  [local_body(): gain_kv.astype(F32)[None, :]]
where the time goes in v2:
time: 69.9 us; the launch traced here: 69.7 us
  Pallas kernels  64.7 us (93%)
  local copies, waits for them, and re-layouts  4.32 us (6%)
    pallas_call x1, Pallas kernels, mla(): pl.pallas_call(functools.partial(body, n_sp, heads, d_model, blk), out_sh...  64.7 us
    unnamed x2, local copies, waits for them, and re-layouts  4.32 us

profile of v2, /device:TPU:81, one launch (start us, length us, event | category | flops | bytes accessed | tf_op | source)
XLA Modules:
  0.0 69.7 jit_solution(6754653258726891673)
XLA Ops:
  0.6 64.7 %mla.1 = (bf16[64,7168]{1,0:T(8,128)(2,1)}, bf16[64,7168]{1,0:T(8,128)(2,1)}) custom-call(bf16[64,7168]{1,0:T(8,128)(2,1)} %x_one.1, bf16[64,7168]{1,0:T(8,128)(2,1)} %x_two.1, s32[64]{0:T(128)} %pos_one.1, s32[64]{0:T(128)} %pos_two.1, f32[1,128]{1,0:T(1,128)} %constant.2.clone.freq, bf16[7168,1536]{1,0:T(8,128)(2,1)} %w_qd.1, bf16[1536]{0:T(1024)(128)(2,1)} %gain_q.1, ...), custom_call_target="tpu_custom_call" | custom-call | tf_op jit(solution)/shard_map/mla/pallas_call | solution.py:464
  65.4 2.2 %copy.16 = bf16[64,7168]{1,0:T(8,128)(2,1)} copy(bf16[64,7168]{1,0:T(8,128)(2,1)} %get-tuple-element.4) | data formatting | bytes 1835008
  67.5 2.2 %copy.17 = bf16[64,7168]{1,0:T(8,128)(2,1)} copy(bf16[64,7168]{1,0:T(8,128)(2,1)} %get-tuple-element.5) | data formatting | bytes 1835008

commit v3 on v2

--- a/solution.py
+++ b/solution.py
@@ -25,7 +25,9 @@
 RING = 25
 WO_RING = 24
 QU_HEADS = 4
-QU_SLOTS = 3
+QU_SLOTS = 2
+RING_QU = 6
+AHEAD = 4
 KU_HEADS = 2
 KU_SLOTS = 4
 KVW = KV_LAT + LANES
@@ -39,8 +41,8 @@
          x_one, x_two, pos_one, pos_two, freq, w_qd, gain_q, w_qu, w_kvd, gain_kv, w_kvu, w_out,
          y_one, y_two,
          x_all, pos_s, ends, pos_all, trig, ring, qu, ku, acc_kv, acc_q, kv_all, cq_all,
-         cap, kr, q_s, kvs0, kvs1, s0, s1, p0, p1, o_all, acc_y, y_st,
-         x_sem, x_ss, x_rs, pos_sem, pos_ss, pos_rs, ring_sem, qd_sem, qu_sem, ku_sem,
+         cap, kr, q_s, f_s, kvs0, kvs1, s0, s1, p0, p1, o_all, y_st,
+         x_sem, x_ss, x_rs, pos_sem, pos_ss, pos_rs, kvd_sem, qd_sem, qu_sem, ku_sem, wo_sem,
          kv_ss, kv_rs, cq_ss, cq_rs, o_ss, o_rs, y_ls, y_ss, y_rs):
     me = lax.axis_index("sp")
     core = lax.rem(me, 2)
@@ -58,9 +60,10 @@
     n_kvd = d_model // COLS
     n_qu = half_heads // QU_HEADS
     n_ku = half_heads // KU_HEADS
-    n_wo_k = heads * V_DIM // ROWS
+    n_wo_k = heads * V_DIM // ROWS // 2
     n_wo_n = y_cols // COLS
-    n_wo = n_wo_k * n_wo_n
+    n_wo = 2 * n_wo_n
+    n_part = WO_RING // n_wo_k
 
     def rcopy(src, dst, ss, rs, dev):
         return pltpu.make_async_remote_copy(
@@ -70,11 +73,11 @@
     def ds(start, size):
         return pl.ds(start if isinstance(start, int) else pl.multiple_of(start, size), size)
 
+    half = COLS // 2
+
     def kvd_copy(k):
         dst = ring.at[k, pl.ds(0, KV_LAT + ROPE_DIM)]
-        return pltpu.make_async_copy(w_kvd.at[:, ds(k * COLS, COLS)], dst, ring_sem.at[k])
-
-    half = COLS // 2
+        return pltpu.make_async_copy(w_kvd.at[:, ds(k * COLS, COLS)], dst, kvd_sem.at[k])
 
     def qd_refs(k):
         return ring.at[n_kvd + k], ring.at[n_kvd + n_down + k // 2, :, ds(lax.rem(k, 2) * half, half)]
@@ -86,11 +89,34 @@
         return (pltpu.make_async_copy(w_qd.at[rows, pl.ds(pl.multiple_of(col, half), COLS)], one, qd_sem.at[k, 0]),
                 pltpu.make_async_copy(w_qd.at[rows, pl.ds(pl.multiple_of(col + COLS, half), half)], two, qd_sem.at[k, 1]))
 
-    def qu_copy(i):
+    low_rows = Q_LAT - ROWS
+
+    def qu_parts(i):
         width = QU_HEADS * QK_DIM
-        cols = ds(core * (half_heads * QK_DIM) + i * width, width)
-        slot = lax.rem(i, QU_SLOTS)
-        return pltpu.make_async_copy(w_qu.at[:, cols], qu.at[slot], qu_sem.at[slot])
+        if i >= RING_QU:
+            return [((0, 0, Q_LAT, width), qu.at[(i - RING_QU) % QU_SLOTS])]
+        rest = width - COLS
+        return [((0, 0, ROWS, COLS), ring.at[3 * i]),
+                ((0, COLS, ROWS, rest), ring.at[3 * i + 1, :, pl.ds(0, rest)]),
+                ((ROWS, 0, low_rows, COLS), ring.at[3 * i + 2, pl.ds(0, low_rows)]),
+                ((ROWS, COLS, low_rows, rest), ring.at[3 * i + 2, pl.ds(low_rows, low_rows), pl.ds(0, rest)])]
+
+    def qu_copies(i):
+        base = core * (half_heads * QK_DIM) + i * (QU_HEADS * QK_DIM)
+        out = []
+        for n, ((r, c, nr, nc), dst) in enumerate(qu_parts(i)):
+            cols = pl.ds(pl.multiple_of(base + c, half), nc)
+            out.append(pltpu.make_async_copy(w_qu.at[pl.ds(r, nr), cols], dst, qu_sem.at[i, n]))
+        return out
+
+    def qu_dot(i):
+        parts = [dst[...] for _, dst in qu_parts(i)]
+        if len(parts) == 1:
+            return jnp.dot(cq_all[...], parts[0], preferred_element_type=F32)
+        top = jnp.concatenate(parts[:2], axis=1)
+        bottom = jnp.concatenate(parts[2:], axis=1)
+        return (jnp.dot(cq_all[:, :ROWS], top, preferred_element_type=F32)
+                + jnp.dot(cq_all[:, ROWS:], bottom, preferred_element_type=F32))
 
     def ku_copy(i):
         width = KU_HEADS * KV_DIM
@@ -98,11 +124,13 @@
         slot = lax.rem(i, KU_SLOTS)
         return pltpu.make_async_copy(w_kvu.at[:, cols], ku.at[slot], ku_sem.at[slot])
 
+    def wo_part(g):
+        return pl.ds(g % n_part * n_wo_k if isinstance(g, int) else lax.rem(g, n_part) * n_wo_k, n_wo_k)
+
     def wo_copy(g):
-        rows = ds(lax.rem(g, n_wo_k) * ROWS, ROWS)
-        cols = ds(core * y_cols + g // n_wo_k * COLS, COLS)
-        slot = lax.rem(g, WO_RING)
-        return pltpu.make_async_copy(w_out.at[rows, cols], ring.at[slot], ring_sem.at[slot])
+        side = lax.rem(core + g, 2)
+        cols = ds(core * y_cols + g // 2 * COLS, COLS)
+        return pltpu.make_async_copy(w_out.at[ds(side * n_wo_k, n_wo_k), :, cols], ring.at[wo_part(g)], wo_sem.at[lax.rem(g, n_part)])
 
     x_in = (x_one, x_two)
 
@@ -116,8 +144,19 @@
     x_cp = [pltpu.make_async_copy(x_in[m], x_all.at[x_rows(m, core)], x_sem.at[m]) for m in range(2)]
     for c in pos_cp + x_cp:
         c.start()
-    for k in range(n_kvd):
-        kvd_copy(k).start()
+    stream = [[kvd_copy(2 * k), kvd_copy(2 * k + 1)] for k in range(n_down)]
+    stream += [qd_copies(k) for k in range(n_down)]
+    stream += [qu_copies(i) for i in range(RING_QU + QU_SLOTS)]
+    issued = []
+
+    def issue(count):
+        for _ in range(count):
+            if len(issued) < len(stream):
+                for c in stream[len(issued)]:
+                    c.start()
+                issued.append(None)
+
+    issue(AHEAD)
 
     barrier = pltpu.get_barrier_semaphore()
     for dev in (pair, left, right):
@@ -154,21 +193,22 @@
     for c in x_cp:
         c.wait()
 
-    acc_kv[...] = jnp.zeros_like(acc_kv)
-
     my_x = ds(core * q_rows, q_rows)
-
-    def kv_step(k, carry):
-        for c in qd_copies(k):
-            c.start()
+    lat_rows = KV_LAT + ROPE_DIM
+    u = [None, None]
+    for k in range(n_down):
         for c in range(2):
             kvd_copy(2 * k + c).wait()
+        issue(3 if k == n_down - 1 else 1)
         x_k = x_all[my_x, ds(k * ROWS, ROWS)]
-        w_k = jnp.concatenate([ring[2 * k, :KV_LAT + ROPE_DIM], ring[2 * k + 1, :KV_LAT + ROPE_DIM]], axis=1)
-        acc_kv[...] += lax.dot_general(x_k, w_k, (((1,), (1,)), ((), ())), preferred_element_type=F32)
-        return carry
-
-    lax.fori_loop(0, n_down, kv_step, 0)
+        for h, (a, b) in enumerate(((0, lat_rows // 2), (lat_rows // 2, lat_rows))):
+            w_k = jnp.concatenate([ring[2 * k, a:b], ring[2 * k + 1, a:b]], axis=1)
+            d = lax.dot_general(w_k, x_k, (((1,), (1,)), ((), ())), preferred_element_type=F32)
+            u[h] = d if k == 0 else u[h] + d
+    acc_kv[:lat_rows // 2, :] = u[0]
+    acc_kv[lat_rows // 2:lat_rows, :] = u[1]
+    acc_kv[lat_rows:, :] = u[1][lat_rows // 2 - ROPE_DIM:, :]
+    lat_all = acc_kv[...].T
     ends_rc.start()
 
     def rotate(z, cos, sin, sel):
@@ -177,12 +217,10 @@
 
     own = ds(me * blk, blk)
     for m in range(2):
-        rows = pl.ds(m * blk, blk)
-        lat = acc_kv[rows, :KV_LAT]
+        lat = lat_all[m * blk:(m + 1) * blk, :KV_LAT]
         inv = lax.rsqrt(jnp.mean(lat * lat, axis=-1, keepdims=True) + NORM_EPS)
         kv_all[m, own, :KV_LAT] = (lat * inv * gain_kv[...].astype(F32).reshape(1, -1)).astype(BF16)
-        raw = acc_kv[rows, KV_LAT:]
-        raw = jnp.concatenate([raw, raw], axis=1)
+        raw = lat_all[m * blk:(m + 1) * blk, KV_LAT:]
         kv_all[m, own, KV_LAT:] = rotate(raw, trig[0, my_rows(m, core), :], trig[1, my_rows(m, core), :], first_half).astype(BF16)
 
     def piece(m, dev):
@@ -202,25 +240,23 @@
         sends.append(kv_send(len(sends), m, me, 0, pair))
     for c in sends:
         c.start()
-    for i in range(QU_SLOTS):
-        qu_copy(i).start(priority=1)
-    for i in range(KU_SLOTS):
-        ku_copy(i).start(priority=1)
-
     for c in x_rc:
         c.wait_recv()
     my_cols = ds(core * q_cols, q_cols)
-    acc_q[:, my_cols] = jnp.zeros((2 * q_rows, q_cols), F32)
-
-    def q_step(k, carry):
+    z = [None, None]
+    for k in range(n_down):
         for c in qd_copies(k):
             c.wait()
+        issue(4 if k == n_down - 1 else 1)
         one, two = qd_refs(k)
         w_k = jnp.concatenate([one[...], two[...]], axis=1)
-        acc_q[:, my_cols] += jnp.dot(x_all[:, ds(k * ROWS, ROWS)], w_k, preferred_element_type=F32)
-        return carry
-
-    lax.fori_loop(0, n_down, q_step, 0)
+        for h in range(2):
+            d = jnp.dot(x_all[h * q_rows:(h + 1) * q_rows, k * ROWS:(k + 1) * ROWS], w_k, preferred_element_type=F32)
+            z[h] = d if k == 0 else z[h] + d
+    for h in range(2):
+        acc_q[h * q_rows:(h + 1) * q_rows, my_cols] = z[h]
+    for i in range(KU_SLOTS):
+        ku_copy(i).start(priority=1)
     cq_rc = rcopy(acc_q.at[:, my_cols], acc_q.at[:, my_cols], cq_ss.at[0], cq_rs.at[0], pair)
     cq_rc.start()
 
@@ -236,6 +272,7 @@
             cap[m, :, c * LANES:(c + 1) * LANES] = jnp.where(keep, BIG, MASKED)
 
     cq_rc.wait_recv()
+    cq_rc.wait_send()
     for m in range(2):
         for c in range(2):
             lat = acc_q[c * q_rows + m * blk:c * q_rows + (m + 1) * blk, :]
@@ -259,37 +296,39 @@
     first_half2 = lax.rem(lane2, ROPE_DIM) < HALF_ROPE
     low = lane2 < ROPE_DIM
 
-    def qu_step(i, carry):
-        qu_copy(i).wait()
-        f = jnp.dot(cq_all[...], qu[lax.rem(i, QU_SLOTS)], preferred_element_type=F32)
-        for p in range(QU_HEADS // 2):
-            base = 2 * QK_DIM * p
-            t0 = f[:, base:base + LANES]
-            t1 = f[:, base + LANES:base + 2 * LANES]
-            t2 = f[:, base + 2 * LANES:base + 3 * LANES]
+    f_buf = (acc_q, f_s)
+    f_width = QU_HEADS * QK_DIM
+
+    def q_post(t):
+        for p in range(QU_HEADS):
+            i, base = 2 * t + p // 2, 2 * QK_DIM * (p % 2)
+            t0, t1, t2 = (f_buf[t % 2][:, 2 * QK_DIM * p + LANES * n:2 * QK_DIM * p + LANES * (n + 1)] for n in range(3))
             q_s[i, :, base:base + LANES] = t0.astype(BF16)
             q_s[i, :, base + LANES:base + 2 * LANES] = pltpu.roll(jnp.where(low, t2, t1), ROPE_DIM, 1).astype(BF16)
             q_s[i, :, base + 2 * LANES:base + 3 * LANES] = rotate(jnp.where(low, t1, t2), trig[0], trig[1], first_half2).astype(BF16)
 
-        @pl.when(i + QU_SLOTS < n_qu)
-        def _():
-            qu_copy(i + QU_SLOTS).start()
-
-        return carry
-
-    n_before = n_qu * 3 // 4
-    lax.fori_loop(0, n_before, qu_step, 0)
-    third = []
-    for m in range(2):
-        kv_wait(m, opp, 3)
-        third.append(kv_send(12 + m, m, opp, 6, pair))
-    for c in third:
-        c.start()
-    sends += third
-    lax.fori_loop(n_before, n_qu, qu_step, 0)
-    n_early = n_wo_k
-    for g in range(n_early):
-        wo_copy(g).start(priority=1)
+    for t in range(n_qu // 2):
+        for i in (2 * t, 2 * t + 1):
+            for c in qu_copies(i):
+                c.wait()
+        for i in (2 * t - 2, 2 * t - 1):
+            if i >= RING_QU and i + QU_SLOTS < n_qu:
+                for c in qu_copies(i + QU_SLOTS):
+                    c.start()
+        if t == n_qu // 2 - 1:
+            third = []
+            for m in range(2):
+                kv_wait(m, opp, 3)
+                third.append(kv_send(12 + m, m, opp, 6, pair))
+            for c in third:
+                c.start()
+            sends += third
+        for h in range(2):
+            f_buf[t % 2][:, h * f_width:(h + 1) * f_width] = qu_dot(2 * t + h)
+        if t > 0:
+            q_post(t - 1)
+    wo_copy(0).start(priority=1)
+    q_post(n_qu // 2 - 1)
 
     other = 1 - 2 * core
     for m in range(2):
@@ -308,8 +347,8 @@
     o_width = 2 * KU_HEADS * V_DIM
 
     def o_copy(t):
-        cols = ds(core * (half_heads * V_DIM) + t * o_width, o_width)
-        return rcopy(o_all.at[:, cols], o_all.at[:, cols], o_ss.at[t], o_rs.at[t], pair)
+        cols = ds(t * o_width, o_width)
+        return rcopy(o_all.at[core, :, cols], o_all.at[core, :, cols], o_ss.at[t], o_rs.at[t], pair)
 
     def kv_up(b, i):
         for m in range(2):
@@ -344,16 +383,14 @@
             for j in range(KU_HEADS):
                 v = kvs[b][m, :, KV_DIM * j + NOPE_DIM:KV_DIM * (j + 1)]
                 o = jnp.dot(p_scr[b][KU_HEADS * m + j], v, preferred_element_type=F32).astype(BF16)
-                col = pl.multiple_of(core * (half_heads * V_DIM) + t * o_width + (KU_HEADS * b + j) * V_DIM, V_DIM)
-                o_all[rows, pl.ds(col, V_DIM)] = o
+                col = t * o_width + (KU_HEADS * b + j) * V_DIM
+                o_all[core, rows, ds(col, V_DIM)] = o
 
     ku_copy(0).wait()
     kv_up(0, 0)
     scores(0, 0)
     ku_copy(KU_SLOTS).start()
     n_loop = n_ku // 2 - 1
-    n_late = WO_RING - n_early
-    per = -(-n_late // n_loop)
 
     def at_step(t, carry):
         ku_copy(2 * t + 1).wait()
@@ -370,12 +407,9 @@
             @pl.when(2 * t + d < n_ku)
             def _():
                 ku_copy(2 * t + d).start()
-        for d in range(per):
-            g = n_early + t * per + d
-
-            @pl.when(g < WO_RING)
-            def _():
-                wo_copy(g).start(priority=1)
+        @pl.when(t + 1 < n_part)
+        def _():
+            wo_copy(t + 1).start(priority=1)
 
         o_copy(t).start()
         return carry
@@ -391,14 +425,10 @@
     values(1, last)
     o_copy(last).start()
 
-    for t in range(n_loop + 1):
-        cols = ds((1 - core) * (half_heads * V_DIM) + t * o_width, o_width)
-        rcopy(o_all.at[:, cols], o_all.at[:, cols], o_ss.at[t], o_rs.at[t], pair).wait_recv()
-
     y_out = (y_one, y_two)
 
     def y_copies(n):
-        slot = lax.rem(n, 2)
+        slot = n % 2
         cols = ds(core * y_cols + n * COLS, COLS)
         local = [pltpu.make_async_copy(y_st.at[slot, my_rows(m, core)], y_out[m].at[:, cols], y_ls.at[slot, m]) for m in range(2)]
         remote = [rcopy(y_st.at[slot, my_rows(m, 1 - core)], y_out[m].at[:, cols], y_ss.at[slot, m], y_rs.at[n, m], pair) for m in range(2)]
@@ -410,37 +440,46 @@
             local[m].wait()
             remote[m].wait_send()
 
-    def wo_step(n, carry):
-        for k in range(n_wo_k):
-            wo_copy(n * n_wo_k + k).wait()
-        first = lax.rem(n * n_wo_k, WO_RING)
-        w_n = ring[pl.ds(first, n_wo_k)].reshape(n_wo_k * ROWS, COLS)
-        acc_y[...] = jnp.dot(o_all[...], w_n, preferred_element_type=F32)
-
-        @pl.when((n + 1) * n_wo_k + WO_RING <= n_wo)
-        def _():
-            for k in range(n_wo_k):
-                wo_copy(n * n_wo_k + WO_RING + k).start()
-
-        @pl.when(n >= 2)
-        def _():
-            y_wait(n - 2)
-
-        y_st[lax.rem(n, 2)] = acc_y[...].astype(BF16)
+    def half_dot(g):
+        side = lax.rem(core + g, 2)
+        w_g = ring[wo_part(g)].reshape(n_wo_k * ROWS, COLS)
+        return jnp.dot(o_all[side], w_g, preferred_element_type=F32)
+
+    def y_start(n):
         local, remote = y_copies(n)
         for m in range(2):
+            remote[m].start()
             local[m].start()
-            remote[m].start()
-        return carry
-
-    lax.fori_loop(0, n_wo_n, wo_step, 0)
+
+    wo_copy(0).wait()
+    acc = half_dot(0)
+    for t in range(n_loop + 1):
+        cols = ds(t * o_width, o_width)
+        rcopy(o_all.at[1 - core, :, cols], o_all.at[1 - core, :, cols], o_ss.at[t], o_rs.at[t], pair).wait_recv()
+    wo_copy(1).wait()
+    acc = acc + half_dot(1)
+    for n in range(1, n_wo_n + 1):
+        if n < n_wo_n:
+            for g in (2 * n, 2 * n + 1):
+                wo_copy(g).wait()
+        if n >= 2:
+            y_start(n - 2)
+        if n >= 3:
+            y_wait(n - 3)
+        for g in (2 * n - 2 + n_part, 2 * n - 1 + n_part):
+            if g < n_wo:
+                wo_copy(g).start()
+        y_st[(n - 1) % 2] = acc.astype(BF16)
+        if n < n_wo_n:
+            acc = half_dot(2 * n) + half_dot(2 * n + 1)
+    y_start(n_wo_n - 1)
     y_wait(n_wo_n - 2)
     y_wait(n_wo_n - 1)
     for n in range(n_wo_n):
         cols = ds((1 - core) * y_cols + n * COLS, COLS)
         for m in range(2):
             rcopy(y_st.at[0, my_rows(m, core)], y_out[m].at[:, cols], y_ss.at[0, m], y_rs.at[n, m], pair).wait_recv()
-    for c in x_rc + [ends_rc, cq_rc]:
+    for c in x_rc + [ends_rc]:
         c.wait_send()
     for c in sends:
         c.wait_send()
@@ -450,7 +489,7 @@
 
 def mla(n_sp, x_one, x_two, pos_one, pos_two, freq, w_qd, gain_q, w_qu, w_kvd, gain_kv, w_kvu, w_out):
     blk, d_model = x_one.shape
-    heads = w_out.shape[0] // V_DIM
+    heads = w_out.shape[0] * w_out.shape[1] // V_DIM
     toks = n_sp * blk
     q_rows = 2 * blk
     n_down = d_model // ROWS
@@ -475,24 +514,24 @@
             pltpu.VMEM((RING, ROWS, COLS), BF16),
             pltpu.VMEM((QU_SLOTS, Q_LAT, QU_HEADS * QK_DIM), BF16),
             pltpu.VMEM((KU_SLOTS, KV_LAT, KU_HEADS * KV_DIM), BF16),
-            pltpu.VMEM((2 * blk, KV_LAT + ROPE_DIM), F32),
+            pltpu.VMEM((KV_LAT + 2 * ROPE_DIM, 2 * blk), F32),
             pltpu.VMEM((2 * q_rows, Q_LAT), F32),
             pltpu.VMEM((2, toks, KVW), BF16),
             pltpu.VMEM((2 * q_rows, Q_LAT), BF16),
             pltpu.VMEM((2, q_rows, toks), F32),
             pltpu.VMEM((2, 2, toks, LANES), BF16),
             pltpu.VMEM((n_qu, 2 * q_rows, QU_HEADS * QK_DIM), BF16),
+            pltpu.VMEM((2 * q_rows, 2 * QU_HEADS * QK_DIM), F32),
             pltpu.VMEM((2, toks, KU_HEADS * KV_DIM), BF16),
             pltpu.VMEM((2, toks, KU_HEADS * KV_DIM), BF16),
             pltpu.VMEM((units, q_rows, toks), F32),
             pltpu.VMEM((units, q_rows, toks), F32),
             pltpu.VMEM((units, q_rows, toks), BF16),
             pltpu.VMEM((units, q_rows, toks), BF16),
-            pltpu.VMEM((2 * q_rows, heads * V_DIM), BF16),
-            pltpu.VMEM((2 * q_rows, COLS), F32),
+            pltpu.VMEM((2, 2 * q_rows, heads // 2 * V_DIM), BF16),
             pltpu.VMEM((2, 2 * q_rows, COLS), BF16),
             dma((2,)), dma((2,)), dma((2,)), dma((2,)), dma((1,)), dma((1,)),
-            dma((RING,)), dma((n_down, 2)), dma((QU_SLOTS,)), dma((KU_SLOTS,)),
+            dma((d_model // COLS,)), dma((n_down, 2)), dma((n_qu, 4)), dma((KU_SLOTS,)), dma((WO_RING,)),
             dma((14,)), dma((7, 2)),
             dma((1,)), dma((1,)),
             dma((n_ku // 2,)), dma((n_ku // 2,)),
@@ -512,6 +551,6 @@
     freq = freq.astype(np.float32)[None, :]
 
     def local_body(x_one, seg_one, pos_one, x_two, seg_two, pos_two, w_qdown, gain_q, w_qup, w_kvdown, gain_kv, w_kvup, w_out):
-        return mla(n_sp, x_one, x_two, pos_one, pos_two, jnp.asarray(freq), w_qdown, gain_q, w_qup, w_kvdown.T, gain_kv, w_kvup, w_out)
+        return mla(n_sp, x_one, x_two, pos_one, pos_two, jnp.asarray(freq), w_qdown, gain_q, w_qup, w_kvdown.T, gain_kv, w_kvup, w_out.reshape(-1, ROWS, w_out.shape[1]))
 
     return jax.shard_map(local_body, mesh=mesh, in_specs=(tok_spec, idx_spec, idx_spec, tok_spec, idx_spec, idx_spec) + (P(),) * 7, out_specs=(tok_spec, tok_spec), check_vma=False)

time: 69.9 us -> 66.1 us (0.946)
  Pallas kernels: 64.7 us -> 61 us
    pallas_call x1, Pallas kernels: 64.7 us -> 61 us  [mla(): pl.pallas_call(functools.partial(body, n_sp, heads, d_model, blk), out_sh...]
where the time goes in v3:
time: 66.1 us; the launch traced here: 65.9 us
  Pallas kernels  61 us (92%)
  local copies, waits for them, and re-layouts  4.32 us (7%)
    pallas_call x1, Pallas kernels, mla(): pl.pallas_call(functools.partial(body, n_sp, heads, d_model, blk), out_sh...  61 us
    unnamed x2, local copies, waits for them, and re-layouts  4.32 us

profile of v3, /device:TPU:81, one launch (start us, length us, event | category | flops | bytes accessed | tf_op | source)
XLA Modules:
  0.0 65.9 jit_solution(772769303039896717)
XLA Ops:
  0.6 61.0 %mla.1 = (bf16[64,7168]{1,0:T(8,128)(2,1)}, bf16[64,7168]{1,0:T(8,128)(2,1)}) custom-call(bf16[64,7168]{1,0:T(8,128)(2,1)} %x_one.1, bf16[64,7168]{1,0:T(8,128)(2,1)} %x_two.1, s32[64]{0:T(128)} %pos_one.1, s32[64]{0:T(128)} %pos_two.1, f32[1,128]{1,0:T(1,128)} %constant.2.clone.freq, bf16[7168,1536]{1,0:T(8,128)(2,1)} %w_qd.1, bf16[1536]{0:T(1024)(128)(2,1)} %gain_q.1, ...), custom_call_target="tpu_custom_call" | custom-call | tf_op jit(solution)/shard_map/mla/pallas_call | solution.py:503
  61.6 2.2 %copy.16 = bf16[64,7168]{1,0:T(8,128)(2,1)} copy(bf16[64,7168]{1,0:T(8,128)(2,1)} %get-tuple-element.4) | data formatting | bytes 1835008
  63.8 2.2 %copy.17 = bf16[64,7168]{1,0:T(8,128)(2,1)} copy(bf16[64,7168]{1,0:T(8,128)(2,1)} %get-tuple-element.5) | data formatting | bytes 1835008

commit v4 on v3

--- a/solution.py
+++ b/solution.py
@@ -543,6 +543,42 @@
     )(x_one, x_two, pos_one, pos_two, freq, w_qd, gain_q, w_qu, w_kvd, gain_kv, w_kvu, w_out)
 
 
+PASS_PARTS = 4
+
+
+def pass_body(one_in, two_in, one_out, two_out, buf, in_sem, out_sem):
+    blk, d_model = one_in.shape
+    width = d_model // PASS_PARTS
+    moves = []
+    for n in range(PASS_PARTS):
+        cols = pl.ds(n * width, width)
+        for m, (src, dst) in enumerate(((one_in, one_out), (two_in, two_out))):
+            moves.append((pltpu.make_async_copy(src.at[:, cols], buf.at[m, n], in_sem.at[m, n]),
+                          pltpu.make_async_copy(buf.at[m, n], dst.at[:, cols], out_sem.at[m, n])))
+    for load, _ in moves:
+        load.start()
+    for load, store in moves:
+        load.wait()
+        store.start()
+    for _, store in moves:
+        store.wait()
+
+
+def pass_on(y_one, y_two):
+    blk, d_model = y_one.shape
+    hbm = pl.BlockSpec(memory_space=pl.ANY)
+    dma = pltpu.SemaphoreType.DMA
+    return pl.pallas_call(
+        pass_body,
+        out_shape=[jax.ShapeDtypeStruct(y_one.shape, y_one.dtype)] * 2,
+        in_specs=[hbm, hbm], out_specs=[hbm, hbm],
+        scratch_shapes=[pltpu.VMEM((2, PASS_PARTS, blk, d_model // PASS_PARTS), BF16),
+                        dma((2, PASS_PARTS)), dma((2, PASS_PARTS))],
+        compiler_params=pltpu.CompilerParams(vmem_limit_bytes=67043328),
+        name="pass_on",
+    )(y_one, y_two)
+
+
 def solution(mesh):
     tok_spec = P(('dp', 'sp'), None)
     idx_spec = P(('dp', 'sp'))
@@ -551,6 +587,7 @@
     freq = freq.astype(np.float32)[None, :]
 
     def local_body(x_one, seg_one, pos_one, x_two, seg_two, pos_two, w_qdown, gain_q, w_qup, w_kvdown, gain_kv, w_kvup, w_out):
-        return mla(n_sp, x_one, x_two, pos_one, pos_two, jnp.asarray(freq), w_qdown, gain_q, w_qup, w_kvdown.T, gain_kv, w_kvup, w_out.reshape(-1, ROWS, w_out.shape[1]))
+        y_one, y_two = mla(n_sp, x_one, x_two, pos_one, pos_two, jnp.asarray(freq), w_qdown, gain_q, w_qup, w_kvdown.T, gain_kv, w_kvup, w_out.reshape(-1, ROWS, w_out.shape[1]))
+        return pass_on(y_one, y_two)
 
     return jax.shard_map(local_body, mesh=mesh, in_specs=(tok_spec, idx_spec, idx_spec, tok_spec, idx_spec, idx_spec) + (P(),) * 7, out_specs=(tok_spec, tok_spec), check_vma=False)

time: 66.1 us -> 64.3 us (0.973)
  local copies, waits for them, and re-layouts: 4.32 us -> 0 us
  Pallas kernels: 61 us -> 63.4 us
    unnamed x2 -> x0, local copies, waits for them, and re-layouts: 4.32 us -> none
    pallas_call x0 -> x1, Pallas kernels: none -> 2.41 us  [pass_on(): pl.pallas_call(pass_body, out_shape=[jax.ShapeDtypeStruct(y_one.shape, y_...]
where the time goes in v4:
time: 64.3 us; the launch traced here: 64.2 us
  Pallas kernels  63.4 us (99%)
  between operations  0.8 us (1%)
    pallas_call x1, Pallas kernels, mla(): pl.pallas_call(functools.partial(body, n_sp, heads, d_model, blk), out_sh...  61 us
    pallas_call x1, Pallas kernels, pass_on(): pl.pallas_call(pass_body, out_shape=[jax.ShapeDtypeStruct(y_one.shape, y_...  2.41 us

profile of v4, /device:TPU:81, one launch (start us, length us, event | category | flops | bytes accessed | tf_op | source)
XLA Modules:
  0.0 64.2 jit_solution(9385522294957854552)
XLA Ops:
  0.6 61.0 %mla.1 = (bf16[64,7168]{1,0:T(8,128)(2,1)}, bf16[64,7168]{1,0:T(8,128)(2,1)}) custom-call(bf16[64,7168]{1,0:T(8,128)(2,1)} %x_one.1, bf16[64,7168]{1,0:T(8,128)(2,1)} %x_two.1, s32[64]{0:T(128)} %pos_one.1, s32[64]{0:T(128)} %pos_two.1, f32[1,128]{1,0:T(1,128)} %constant.2.clone.freq, bf16[7168,1536]{1,0:T(8,128)(2,1)} %w_qd.1, bf16[1536]{0:T(1024)(128)(2,1)} %gain_q.1, ...), custom_call_target="tpu_custom_call" | custom-call | tf_op jit(solution)/shard_map/mla/pallas_call | solution.py:503
  61.6 2.4 %pass_on.1 = (bf16[64,7168]{1,0:T(8,128)(2,1)}, bf16[64,7168]{1,0:T(8,128)(2,1)}) custom-call(bf16[64,7168]{1,0:T(8,128)(2,1)} %get-tuple-element.4.one_in, bf16[64,7168]{1,0:T(8,128)(2,1)} %get-tuple-element.5.two_in), custom_call_target="tpu_custom_call" | custom-call | tf_op jit(solution)/shard_map/pass_on/pallas_call | solution.py:571
